TPU v7x, 32 devices: a whole 2x2x4 slice. The times are simulated.
32 devices in a mesh: tm: 2 (over x), gx: 4 (over z), gy: 4 (over y, core).
Axes of the slice: x: 2, y: 2, z: 4, core: 2. Of those that a mesh axis runs over, the one named last changes fastest.
Arguments:
- increment: float32 [2, 137, 64, 512], P('tm', None, 'gx', 'gy'), may hold values from -6 to 6
- dual_state: float32 [2, 137, 64, 512], P('tm', None, 'gx', 'gy'), may hold values from -6 to 6
- forcing: float32 [2, 137, 64, 512], P('tm', None, 'gx', 'gy'), may hold values from -6 to 6
- gradient: float32 [2, 137, 64, 512], P('tm', None, 'gx', 'gy'), may hold values from -3 to 3
- courant_x: float32 [2, 137, 64, 512], P('tm', None, 'gx', 'gy'), may hold values from 0.05 to 0.3
- courant_y: float32 [2, 137, 64, 512], P('tm', None, 'gx', 'gy'), may hold values from 0.05 to 0.3
- error_var: float32 [2, 137, 64, 512], P('tm', None, 'gx', 'gy'), may hold values from 0.2 to 2
- obs_weight: float32 [2, 137, 64, 512], P('tm', None, 'gx', 'gy'), may hold values from 0.2 to 2
- diffusion: float32 [137], replicated, may hold values from 0.02 to 0.1
- level_mix: float32 [137, 137], replicated, may hold values from -0.5 to 0.8
Outputs:
- dual_next: float32 [2, 137, 64, 512], P('tm', None, 'gx', 'gy')
- increment_next: float32 [2, 137, 64, 512], P('tm', None, 'gx', 'gy')
All inputs are finite; a program needn't handle non-finite values.
Results may differ from a plain program's by a relative error of at most 0.0001.
Values sent between devices are 32-bit elements; how exact they have to be, the bound alone decides.
A program may use at most 128 MiB of HBM per device.

v0:
```python
import functools

import jax
import jax.numpy as jnp
from jax import lax
from jax.experimental import pallas as pl
from jax.experimental.pallas import tpu as pltpu
from jax.sharding import PartitionSpec as P

STEPS = 3


def shifted(block, axis, distance):
    devices = range(lax.axis_size(axis))
    route = [(i - distance, i) for i in devices if i - distance in devices]
    return lax.ppermute(block, axis, route)


def summed(value, axis):
    count = lax.axis_size(axis)
    if count & (count - 1):
        return lax.psum(value, axis)
    bit = 1
    while bit < count:
        value = value + lax.ppermute(value, axis, [(i, i ^ bit) for i in range(count)])
        bit *= 2
    return value


def split(block):
    high = block.astype(jnp.bfloat16)
    return high, (block - high.astype(jnp.float32)).astype(jnp.bfloat16)


def mixed(high, low, block):
    block_high, block_low = split(block)
    dot = functools.partial(jnp.dot, preferred_element_type=jnp.float32)
    return dot(high, block_low) + dot(low, block_high) + dot(high, block_high)


def kernel(
    adjoint, stencil, mix, v, x_low, x_high, y_low, y_high, a, b, a_low, b_low, s, matrix, out
):
    rows, levels, width = v.shape
    high, low = split(matrix[...])
    lane = lax.broadcasted_iota(jnp.int32, (levels, width), 1)

    def row(i):
        current = v[i]
        if not stencil:
            return current
        spread = s[...]
        minus_x = v[i - 1] if i else x_low[0]
        plus_x = v[i + 1] if i < rows - 1 else x_high[0]
        minus_y = jnp.where(lane == 0, y_low[i], pltpu.roll(current, 1, 1))
        plus_y = jnp.where(lane == width - 1, y_high[i], pltpu.roll(current, width - 1, 1))
        flow_x, flow_y = a[i], b[i]
        result = (1.0 - flow_x - flow_y - 4.0 * spread) * current
        if adjoint:
            result = result + flow_x * plus_x + flow_y * plus_y
        else:
            lower_x = a[i - 1] if i else a_low[0]
            lower_y = jnp.where(lane == 0, b_low[i], pltpu.roll(flow_y, 1, 1))
            result = result + lower_x * minus_x + lower_y * minus_y
        return result + spread * (minus_x + plus_x + minus_y + plus_y)

    group = 2 if rows % 2 == 0 else 1
    for i in range(0, rows, group):
        parts = [row(i + k) for k in range(group)]
        if mix:
            block = jnp.concatenate(parts, axis=1) if group > 1 else parts[0]
            result = mixed(high, low, block)
            parts = [result[:, k * width : (k + 1) * width] for k in range(group)]
        for k in range(group):
            out[i + k] = parts[k]


def step(adjoint, stencil, mix, *operands):
    state = operands[0]
    flops = 2 * 3 * state.size * state.shape[1]
    return pl.pallas_call(
        functools.partial(kernel, adjoint, stencil, mix),
        out_shape=jax.ShapeDtypeStruct(state.shape, state.dtype),
        in_specs=[pl.BlockSpec(memory_space=pltpu.VMEM)] * len(operands),
        out_specs=pl.BlockSpec(memory_space=pltpu.VMEM),
        compiler_params=pltpu.CompilerParams(vmem_limit_bytes=40 * 1024 * 1024),
        cost_estimate=pl.CostEstimate(
            flops=flops, bytes_accessed=16 * state.size, transcendentals=0
        ),
    )(*operands)


def rims(state):
    x_low = shifted(state[-1:], "gx", 1)
    x_high = shifted(state[:1], "gx", -1)
    y_low = shifted(state[:, :, -1], "gy", 1)[:, :, None]
    y_high = shifted(state[:, :, 0], "gy", -1)[:, :, None]
    return x_low, x_high, y_low, y_high


def local(
    increment,
    dual_state,
    forcing,
    gradient,
    courant_x,
    courant_y,
    error_var,
    obs_weight,
    diffusion,
    level_mix,
):
    initial = increment[0]
    dual_now = dual_state[0]
    later = shifted(dual_now, "tm", -1)
    forward, backward, flow_x, flow_y = (
        jnp.swapaxes(part, 0, 1) for part in (initial, later, courant_x[0], courant_y[0])
    )
    a_low = shifted(flow_x[-1:], "gx", 1)
    b_low = shifted(flow_y[:, :, -1], "gy", 1)[:, :, None]
    flows = (flow_x, flow_y, a_low, b_low, diffusion[:, None])
    back = level_mix.T
    zeros = tuple(jnp.zeros_like(part) for part in (a_low, a_low, b_low, b_low))
    backward = step(True, False, True, backward, *zeros, *flows, back)
    for substep in range(STEPS):
        forward = step(False, True, True, forward, *rims(forward), *flows, level_mix)
        last = substep == STEPS - 1
        backward = step(True, True, not last, backward, *rims(backward), *flows, back)
    forward_state = jnp.swapaxes(forward, 0, 1)
    adjoint_state = jnp.swapaxes(backward, 0, 1)
    earlier_end = shifted(forward_state, "tm", 1)
    residual_dual = forcing[0] - error_var[0] * dual_now - initial + earlier_end
    residual_incr = gradient[0] - obs_weight[0] * initial - dual_now + adjoint_state
    squares = jnp.sum(residual_dual * residual_dual) + jnp.sum(residual_incr * residual_incr)
    global_sum = squares
    for axis in ("gy", "gx", "tm"):
        global_sum = summed(global_sum, axis)
    cell_count = (
        2 * residual_dual.size * lax.axis_size("tm") * lax.axis_size("gx") * lax.axis_size("gy")
    )
    root_mean = jnp.sqrt(global_sum / cell_count + 1e-06)
    step_scale = jnp.minimum(1.0, 0.5 / root_mean)
    dual_next = dual_now + step_scale * residual_dual
    increment_next = initial + step_scale * residual_incr
    return (dual_next[None], increment_next[None])


def solution(mesh):
    in_specs = (
        P("tm", None, "gx", "gy"),
        P("tm", None, "gx", "gy"),
        P("tm", None, "gx", "gy"),
        P("tm", None, "gx", "gy"),
        P("tm", None, "gx", "gy"),
        P("tm", None, "gx", "gy"),
        P("tm", None, "gx", "gy"),
        P("tm", None, "gx", "gy"),
        P(),
        P(),
    )
    out_specs = (P("tm", None, "gx", "gy"), P("tm", None, "gx", "gy"))
    return jax.shard_map(local, mesh=mesh, in_specs=in_specs, out_specs=out_specs, check_vma=False)
```

profile of v0, /device:TPU:0, one launch (start us, length us, event | category | flops | bytes accessed | tf_op | source)
XLA Modules:
  0.0 228.6 jit_solution(15098967152187311033)
XLA Ops:
  2.1 1.6 copy.182
  4.3 5.7 %collective-permute-start.4 = (f32[1,137,128]{2,1,0:T(8,128)}, f32[1,137,128]{2,1,0:T(8,128)}, u32[]{:S(2)}, u32[]{:S(2)}) collective-permute-start(f32[1,137,128]{2,1,0:T(8,128)} %slice.108), channel_id=1, source_target_pairs={{0,4},{4,8},{8,12},{1,5},{5,9},{9,13},{2,6},{6,10},{10,14},{3,7},{... | collective-permute-start | bytes 210440 | tf_op jit(solution)/shard_map/ppermute | solution.py:16
  14.0 3.5 %collective-permute-start = (f32[1,137,128]{2,1,0:T(8,128)}, f32[1,137,128]{2,1,0:T(8,128)}, u32[]{:S(2)}, u32[]{:S(2)}) collective-permute-start(f32[1,137,128]{2,1,0:T(8,128)} %get-tuple-element.39), channel_id=1, source_target_pairs={{0,4},{4,8},{8,12},{1,5},{5,9},{9,13},{2,6},{6,10},{10,14},{3,7},{... | collective-permute-start | bytes 210440 | tf_op jit(solution)/shard_map/ppermute | solution.py:16
  18.9 1.5 slice_reduce_fusion.11
  20.4 3.7 %collective-permute-start.2 = (f32[16,137]{1,0:T(8,128)S(1)}, f32[16,137]{1,0:T(8,128)S(1)}, u32[]{:S(2)}, u32[]{:S(2)}) collective-permute-start(f32[16,137]{1,0:T(8,128)S(1)} %get-tuple-element.21), channel_id=1, source_target_pairs={{0,1},{1,2},{2,3},{4,5},{5,6},{6,7},{8,9},{9,10},{10,11},{12,13},{... | collective-permute-start | bytes 26312 | tf_op jit(solution)/shard_map/ppermute | solution.py:16
  27.5 2.2 copy.120.y_low
  29.7 2.2 copy.121.y_high
  37.5 3.7 %shard_map.113.v = f32[16,137,128]{2,1,0:T(8,128)S(1)} custom-call(f32[16,137,128]{2,1,0:T(8,128)S(1)} %bitcast.99, f32[1,137,128]{2,1,0:T(8,128)} %collective-permute-done.x_low, f32[1,137,128]{2,1,0:T(8,128)} %collective-permute-done.1.x_high, f32[16,137,1]{2,1,0:T(8,128)S(1)} %copy-done.13, f32[16,137,1]{2,1,0:T(8,128)S(1)} %copy-done.19, ...), custom_call_target="tpu_custom_call" | custom-call | flops 230633472 | bytes 4489216 | tf_op jit(solution)/shard_map/pallas_call | solution.py:81
  41.9 4.9 %collective-permute-start.6 = (f32[1,137,128]{2,1,0:T(8,128)}, f32[1,137,128]{2,1,0:T(8,128)}, u32[]{:S(2)}, u32[]{:S(2)}) collective-permute-start(f32[1,137,128]{2,1,0:T(8,128)} %get-tuple-element.37), channel_id=1, source_target_pairs={{0,4},{4,8},{8,12},{1,5},{5,9},{9,13},{2,6},{6,10},{10,14},{3,7},{... | collective-permute-start | bytes 210440 | tf_op jit(solution)/shard_map/ppermute | solution.py:16
  48.1 1.5 slice_reduce_fusion.8
  49.6 3.4 %collective-permute-start.8 = (f32[16,137]{1,0:T(8,128)S(1)}, f32[16,137]{1,0:T(8,128)S(1)}, u32[]{:S(2)}, u32[]{:S(2)}) collective-permute-start(f32[16,137]{1,0:T(8,128)S(1)} %get-tuple-element.19), channel_id=1, source_target_pairs={{0,1},{1,2},{2,3},{4,5},{5,6},{6,7},{8,9},{9,10},{10,11},{12,13},{... | collective-permute-start | bytes 26312 | tf_op jit(solution)/shard_map/ppermute | solution.py:16
  54.9 2.2 copy.124.y_low
  57.7 2.2 copy.125.y_high
  65.5 3.7 %shard_map.114.v = f32[16,137,128]{2,1,0:T(8,128)S(1)} custom-call(f32[16,137,128]{2,1,0:T(8,128)S(1)} %copy-done.7, f32[1,137,128]{2,1,0:T(8,128)} %collective-permute-done.6.x_low, f32[1,137,128]{2,1,0:T(8,128)} %collective-permute-done.7.x_high, f32[16,137,1]{2,1,0:T(8,128)S(1)} %copy-done.15, f32[16,137,1]{2,1,0:T(8,128)S(1)} %copy-done.20, ...), custom_call_target="tpu_custom_call" | custom-call | flops 230633472 | bytes 4489216 | tf_op jit(solution)/shard_map/pallas_call | solution.py:81
  69.9 5.2 %collective-permute-start.10 = (f32[1,137,128]{2,1,0:T(8,128)}, f32[1,137,128]{2,1,0:T(8,128)}, u32[]{:S(2)}, u32[]{:S(2)}) collective-permute-start(f32[1,137,128]{2,1,0:T(8,128)} %get-tuple-element.35), channel_id=1, source_target_pairs={{0,4},{4,8},{8,12},{1,5},{5,9},{9,13},{2,6},{6,10},{10,14},{3,7},{... | collective-permute-start | bytes 210440 | tf_op jit(solution)/shard_map/ppermute | solution.py:16
  76.6 2.1 slice_reduce_fusion.6
  78.6 4.7 %collective-permute-start.12 = (f32[16,137]{1,0:T(8,128)}, f32[16,137]{1,0:T(8,128)}, u32[]{:S(2)}, u32[]{:S(2)}) collective-permute-start(f32[16,137]{1,0:T(8,128)} %get-tuple-element.17), channel_id=1, source_target_pairs={{0,1},{1,2},{2,3},{4,5},{5,6},{6,7},{8,9},{9,10},{10,11},{12,13},{... | collective-permute-start | bytes 26312 | tf_op jit(solution)/shard_map/ppermute | solution.py:16
  84.6 1.7 copy.138
  86.3 2.2 copy.128.y_low
  88.5 2.2 copy.129.y_high
  96.3 3.8 %shard_map.115 = f32[16,137,128]{2,1,0:T(8,128)S(1)} custom-call(f32[16,137,128]{2,1,0:T(8,128)S(1)} %copy-done.5, f32[1,137,128]{2,1,0:T(8,128)} %collective-permute-done.10.x_low, f32[1,137,128]{2,1,0:T(8,128)} %collective-permute-done.11.x_high, f32[16,137,1]{2,1,0:T(8,128)S(1)} %copy-done.16, f32[16,137,1]{2,1,0:T(8,128)S(1)} %copy-done.21, ...), custom_call_target="tpu_custom_call" | custom-call | flops 230633472 | bytes 4489216 | tf_op jit(solution)/shard_map/pallas_call | solution.py:81
  101.5 6.6 %collective-permute-start.14 = (f32[137,16,128]{2,1,0:T(8,128)}, f32[137,16,128]{2,1,0:T(8,128)}, u32[]{:S(2)}, u32[]{:S(2)}) collective-permute-start(f32[137,16,128]{2,1,0:T(8,128)} %copy.132), channel_id=1, source_target_pairs={{0,16},{1,17},{2,18},{3,19},{4,20},{5,21},{6,22},{7,23},{8,24},{9,... | collective-permute-start | bytes 3366920 | tf_op jit(solution)/shard_map/ppermute | solution.py:16
  108.0 1.6 copy.180
  110.6 1.5 shard_map.116.v
  112.8 4.9 %collective-permute-start.16 = (f32[1,137,128]{2,1,0:T(8,128)}, f32[1,137,128]{2,1,0:T(8,128)}, u32[]{:S(2)}, u32[]{:S(2)}) collective-permute-start(f32[1,137,128]{2,1,0:T(8,128)} %get-tuple-element.33), channel_id=1, source_target_pairs={{0,4},{4,8},{8,12},{1,5},{5,9},{9,13},{2,6},{6,10},{10,14},{3,7},{... | collective-permute-start | bytes 210440 | tf_op jit(solution)/shard_map/ppermute | solution.py:16
  120.5 3.3 %collective-permute-start.18 = (f32[16,137]{1,0:T(8,128)S(1)}, f32[16,137]{1,0:T(8,128)S(1)}, u32[]{:S(2)}, u32[]{:S(2)}) collective-permute-start(f32[16,137]{1,0:T(8,128)S(1)} %get-tuple-element.15), channel_id=1, source_target_pairs={{0,1},{1,2},{2,3},{4,5},{5,6},{6,7},{8,9},{9,10},{10,11},{12,13},{... | collective-permute-start | bytes 26312 | tf_op jit(solution)/shard_map/ppermute | solution.py:16
  125.7 2.2 copy.141.y_low
  128.8 2.2 copy.142.y_high
  136.6 3.0 %shard_map.117.v = f32[16,137,128]{2,1,0:T(8,128)S(1)} custom-call(f32[16,137,128]{2,1,0:T(8,128)S(1)} %copy-done.11, f32[1,137,128]{2,1,0:T(8,128)} %collective-permute-done.16.x_low, f32[1,137,128]{2,1,0:T(8,128)} %collective-permute-done.17.x_high, f32[16,137,1]{2,1,0:T(8,128)S(1)} %copy-done.17, f32[16,137,1]{2,1,0:T(8,128)S(1)} %copy-done.22, ...), custom_call_target="tpu_custom_call" | custom-call | flops 230633472 | bytes 4489216 | tf_op jit(solution)/shard_map/pallas_call | solution.py:81
  140.4 5.2 %collective-permute-start.20 = (f32[1,137,128]{2,1,0:T(8,128)}, f32[1,137,128]{2,1,0:T(8,128)}, u32[]{:S(2)}, u32[]{:S(2)}) collective-permute-start(f32[1,137,128]{2,1,0:T(8,128)} %get-tuple-element.31), channel_id=1, source_target_pairs={{0,4},{4,8},{8,12},{1,5},{5,9},{9,13},{2,6},{6,10},{10,14},{3,7},{... | collective-permute-start | bytes 210440 | tf_op jit(solution)/shard_map/ppermute | solution.py:16
  148.3 4.1 %collective-permute-start.22 = (f32[16,137]{1,0:T(8,128)S(1)}, f32[16,137]{1,0:T(8,128)S(1)}, u32[]{:S(2)}, u32[]{:S(2)}) collective-permute-start(f32[16,137]{1,0:T(8,128)S(1)} %get-tuple-element.13), channel_id=1, source_target_pairs={{0,1},{1,2},{2,3},{4,5},{5,6},{6,7},{8,9},{9,10},{10,11},{12,13},{... | collective-permute-start | bytes 26312 | tf_op jit(solution)/shard_map/ppermute | solution.py:16
  152.4 1.5 collective-permute-start.23
  154.5 2.2 copy.145.y_low
  156.7 2.2 copy.146.y_high
  164.6 3.0 %shard_map.118.v = f32[16,137,128]{2,1,0:T(8,128)S(1)} custom-call(f32[16,137,128]{2,1,0:T(8,128)S(1)} %copy-done.9, f32[1,137,128]{2,1,0:T(8,128)} %collective-permute-done.20.x_low, f32[1,137,128]{2,1,0:T(8,128)} %collective-permute-done.21.x_high, f32[16,137,1]{2,1,0:T(8,128)S(1)} %copy-done.18, f32[16,137,1]{2,1,0:T(8,128)S(1)} %copy-done.23, ...), custom_call_target="tpu_custom_call" | custom-call | flops 230633472 | bytes 4489216 | tf_op jit(solution)/shard_map/pallas_call | solution.py:81
  168.3 5.2 %collective-permute-start.24 = (f32[1,137,128]{2,1,0:T(8,128)}, f32[1,137,128]{2,1,0:T(8,128)}, u32[]{:S(2)}, u32[]{:S(2)}) collective-permute-start(f32[1,137,128]{2,1,0:T(8,128)} %get-tuple-element.29), channel_id=1, source_target_pairs={{0,4},{4,8},{8,12},{1,5},{5,9},{9,13},{2,6},{6,10},{10,14},{3,7},{... | collective-permute-start | bytes 210440 | tf_op jit(solution)/shard_map/ppermute | solution.py:16
  176.3 4.1 %collective-permute-start.26 = (f32[16,137]{1,0:T(8,128)S(1)}, f32[16,137]{1,0:T(8,128)S(1)}, u32[]{:S(2)}, u32[]{:S(2)}) collective-permute-start(f32[16,137]{1,0:T(8,128)S(1)} %get-tuple-element.11), channel_id=1, source_target_pairs={{0,1},{1,2},{2,3},{4,5},{5,6},{6,7},{8,9},{9,10},{10,11},{12,13},{... | collective-permute-start | bytes 26312 | tf_op jit(solution)/shard_map/ppermute | solution.py:16
  182.2 2.2 copy.149.y_low
  184.9 2.2 copy.150.y_high
  192.7 2.8 %shard_map.119 = f32[16,137,128]{2,1,0:T(8,128)S(1)} custom-call(f32[16,137,128]{2,1,0:T(8,128)S(1)} %copy-done.3, f32[1,137,128]{2,1,0:T(8,128)} %collective-permute-done.24.x_low, f32[1,137,128]{2,1,0:T(8,128)} %collective-permute-done.25.x_high, f32[16,137,1]{2,1,0:T(8,128)S(1)} %copy-done.12, f32[16,137,1]{2,1,0:T(8,128)S(1)} %copy-done.14, ...), custom_call_target="tpu_custom_call" | custom-call | flops 230633472 | bytes 4489216 | tf_op jit(solution)/shard_map/pallas_call | solution.py:81
  195.7 4.2 %multiply_reduce_fusion = (f32[]{:T(128)}, f32[137,16,128]{2,0,1:T(8,128)S(1)}, f32[]{:T(128)}, f32[137,16,128]{2,0,1:T(8,128)S(1)}) fusion(f32[16,137,128]{2,1,0:T(8,128)S(1)} %shard_map.119, f32[1,137,16,128]{3,2,1,0:T(8,128)S(1)} %copy-done.40, f32[1,137,16,128]{3,2,1,0:T(8,128)S(1)} %copy-done.38, f32[1,137,16,128]{3,2,1,0:T(8,128)S(1)} %copy-done.41, ...), kind=kLoop, calls=%fused_computation.28 | loop fusion | flops 3366910 | bytes 11223048 | tf_op jit(solution)/shard_map/reduce_sum | solution.py:134
  201.3 3.3 %collective-permute-start.28 = (f32[]{:T(128)}, f32[]{:T(128)}, u32[]{:S(2)}, u32[]{:S(2)}) collective-permute-start(f32[]{:T(128)} %add.35), channel_id=1, source_target_pairs={{0,1},{1,0},{2,3},{3,2},{4,5},{5,4},{6,7},{7,6},{8,9},{9,8},{10,11... | collective-permute-start | bytes 20 | tf_op jit(solution)/shard_map/ppermute | solution.py:25
  205.3 2.9 %collective-permute-start.29 = (f32[]{:T(128)}, f32[]{:T(128)}, u32[]{:S(2)}, u32[]{:S(2)}) collective-permute-start(f32[]{:T(128)} %add.36), channel_id=1, source_target_pairs={{0,2},{1,3},{2,0},{3,1},{4,6},{5,7},{6,4},{7,5},{8,10},{9,11},{10,... | collective-permute-start | bytes 20 | tf_op jit(solution)/shard_map/ppermute | solution.py:25
  209.5 4.0 %collective-permute-start.30 = (f32[]{:T(128)}, f32[]{:T(128)}, u32[]{:S(2)}, u32[]{:S(2)}) collective-permute-start(f32[]{:T(128)} %add.37), channel_id=1, source_target_pairs={{0,4},{4,0},{8,12},{12,8},{1,5},{5,1},{9,13},{13,9},{2,6},{6,2},{1... | collective-permute-start | bytes 20 | tf_op jit(solution)/shard_map/ppermute | solution.py:25
  214.4 2.2 collective-permute-start.31
  216.6 2.3 collective-permute-done.31
  221.0 2.2 collective-permute-done.32
  223.9 2.0 fusion.3
  (169 shorter events, 75.7 us)
Async XLA Ops:
  0.6 9.4 %copy-start.45 = (f32[1,137,16,128]{3,2,1,0:T(8,128)S(1)}, f32[1,137,16,128]{3,2,1,0:T(8,128)}, u32[]{:S(2)}) copy-start(f32[1,137,16,128]{3,2,1,0:T(8,128)} %param.15) | copy-start | bytes 3366916
  0.6 107.4 %collective-permute-start.15 = (f32[137,16,128]{2,1,0:T(8,128)}, f32[137,16,128]{2,1,0:T(8,128)}, u32[]{:S(2)}, u32[]{:S(2)}) collective-permute-start(f32[137,16,128]{2,1,0:T(8,128)} %bitcast.106), channel_id=1, source_target_pairs={{16,0},{17,1},{18,2},{19,3},{20,4},{21,5},{22,6},{23,7},{24,8},{25... | collective-permute-start | bytes 3366920 | tf_op jit(solution)/shard_map/ppermute | solution.py:16
  4.3 8.5 %copy-start.37 = (f32[1,137,16,128]{3,2,1,0:T(8,128)S(1)}, f32[1,137,16,128]{3,2,1,0:T(8,128)}, u32[]{:S(2)}) copy-start(f32[1,137,16,128]{3,2,1,0:T(8,128)} %param.10) | copy-start | bytes 3366916
  4.3 27.5 %collective-permute-start.4 = (f32[1,137,128]{2,1,0:T(8,128)}, f32[1,137,128]{2,1,0:T(8,128)}, u32[]{:S(2)}, u32[]{:S(2)}) collective-permute-start(f32[1,137,128]{2,1,0:T(8,128)} %slice.108), channel_id=1, source_target_pairs={{0,4},{4,8},{8,12},{1,5},{5,9},{9,13},{2,6},{6,10},{10,14},{3,7},{... | collective-permute-start | bytes 210440 | tf_op jit(solution)/shard_map/ppermute | solution.py:16
  11.4 9.1 %collective-permute-start.5 = (f32[16,137]{1,0:T(8,128)S(1)}, f32[16,137]{1,0:T(8,128)S(1)}, u32[]{:S(2)}, u32[]{:S(2)}) collective-permute-start(f32[16,137]{1,0:T(8,128)S(1)} %slice_reduce_fusion.10), channel_id=1, source_target_pairs={{0,1},{1,2},{2,3},{4,5},{5,6},{6,7},{8,9},{9,10},{10,11},{12,13},{... | collective-permute-start | bytes 26312 | tf_op jit(solution)/shard_map/ppermute | solution.py:16
  13.2 7.2 %copy-start = (f32[1,137,16,128]{3,1,2,0:T(8,128)}, f32[1,137,16,128]{3,1,2,0:T(8,128)S(1)}, u32[]{:S(2)}) copy-start(f32[1,137,16,128]{3,1,2,0:T(8,128)S(1)} %copy.183) | copy-start | bytes 3366916
  14.0 17.9 %collective-permute-start = (f32[1,137,128]{2,1,0:T(8,128)}, f32[1,137,128]{2,1,0:T(8,128)}, u32[]{:S(2)}, u32[]{:S(2)}) collective-permute-start(f32[1,137,128]{2,1,0:T(8,128)} %get-tuple-element.39), channel_id=1, source_target_pairs={{0,4},{4,8},{8,12},{1,5},{5,9},{9,13},{2,6},{6,10},{10,14},{3,7},{... | collective-permute-start | bytes 210440 | tf_op jit(solution)/shard_map/ppermute | solution.py:16
  17.5 8.8 %copy-start.51 = (f32[137]{0:T(256)S(1)}, f32[137]{0:T(256)}, u32[]{:S(2)}) copy-start(f32[137]{0:T(256)} %param.18) | copy-start | bytes 1648
  17.5 14.4 %collective-permute-start.1 = (f32[1,137,128]{2,1,0:T(8,128)}, f32[1,137,128]{2,1,0:T(8,128)}, u32[]{:S(2)}, u32[]{:S(2)}) collective-permute-start(f32[1,137,128]{2,1,0:T(8,128)} %get-tuple-element.38), channel_id=1, source_target_pairs={{4,0},{8,4},{12,8},{5,1},{9,5},{13,9},{6,2},{10,6},{14,10},{7,3},{... | collective-permute-start | bytes 210440 | tf_op jit(solution)/shard_map/ppermute | solution.py:16
  20.4 4.5 %collective-permute-start.2 = (f32[16,137]{1,0:T(8,128)S(1)}, f32[16,137]{1,0:T(8,128)S(1)}, u32[]{:S(2)}, u32[]{:S(2)}) collective-permute-start(f32[16,137]{1,0:T(8,128)S(1)} %get-tuple-element.21), channel_id=1, source_target_pairs={{0,1},{1,2},{2,3},{4,5},{5,6},{6,7},{8,9},{9,10},{10,11},{12,13},{... | collective-permute-start | bytes 26312 | tf_op jit(solution)/shard_map/ppermute | solution.py:16
  25.0 4.7 %collective-permute-start.3 = (f32[16,137]{1,0:T(8,128)}, f32[16,137]{1,0:T(8,128)}, u32[]{:S(2)}, u32[]{:S(2)}) collective-permute-start(f32[16,137]{1,0:T(8,128)} %get-tuple-element.20), channel_id=1, source_target_pairs={{1,0},{2,1},{3,2},{5,4},{6,5},{7,6},{9,8},{10,9},{11,10},{13,12},{... | collective-permute-start | bytes 26312 | tf_op jit(solution)/shard_map/ppermute | solution.py:16
  41.2 8.4 %copy-start.6 = (f32[16,137,128]{2,1,0:T(8,128)}, f32[16,137,128]{2,1,0:T(8,128)S(1)}, u32[]{:S(2)}) copy-start(f32[16,137,128]{2,1,0:T(8,128)S(1)} %shard_map.113.v) | copy-start | bytes 3366916
  41.9 18.0 %collective-permute-start.6 = (f32[1,137,128]{2,1,0:T(8,128)}, f32[1,137,128]{2,1,0:T(8,128)}, u32[]{:S(2)}, u32[]{:S(2)}) collective-permute-start(f32[1,137,128]{2,1,0:T(8,128)} %get-tuple-element.37), channel_id=1, source_target_pairs={{0,4},{4,8},{8,12},{1,5},{5,9},{9,13},{2,6},{6,10},{10,14},{3,7},{... | collective-permute-start | bytes 210440 | tf_op jit(solution)/shard_map/ppermute | solution.py:16
  46.8 13.1 %collective-permute-start.7 = (f32[1,137,128]{2,1,0:T(8,128)}, f32[1,137,128]{2,1,0:T(8,128)}, u32[]{:S(2)}, u32[]{:S(2)}) collective-permute-start(f32[1,137,128]{2,1,0:T(8,128)} %get-tuple-element.36), channel_id=1, source_target_pairs={{4,0},{8,4},{12,8},{5,1},{9,5},{13,9},{6,2},{10,6},{14,10},{7,3},{... | collective-permute-start | bytes 210440 | tf_op jit(solution)/shard_map/ppermute | solution.py:16
  49.6 4.7 %collective-permute-start.8 = (f32[16,137]{1,0:T(8,128)S(1)}, f32[16,137]{1,0:T(8,128)S(1)}, u32[]{:S(2)}, u32[]{:S(2)}) collective-permute-start(f32[16,137]{1,0:T(8,128)S(1)} %get-tuple-element.19), channel_id=1, source_target_pairs={{0,1},{1,2},{2,3},{4,5},{5,6},{6,7},{8,9},{9,10},{10,11},{12,13},{... | collective-permute-start | bytes 26312 | tf_op jit(solution)/shard_map/ppermute | solution.py:16
  53.0 4.7 %collective-permute-start.9 = (f32[16,137]{1,0:T(8,128)S(1)}, f32[16,137]{1,0:T(8,128)}, u32[]{:S(2)}, u32[]{:S(2)}) collective-permute-start(f32[16,137]{1,0:T(8,128)S(1)} %get-tuple-element.18), channel_id=1, source_target_pairs={{1,0},{2,1},{3,2},{5,4},{6,5},{7,6},{9,8},{10,9},{11,10},{13,12},{... | collective-permute-start | bytes 26312 | tf_op jit(solution)/shard_map/ppermute | solution.py:16
  69.2 9.4 %copy-start.4 = (f32[16,137,128]{2,1,0:T(8,128)}, f32[16,137,128]{2,1,0:T(8,128)S(1)}, u32[]{:S(2)}) copy-start(f32[16,137,128]{2,1,0:T(8,128)S(1)} %shard_map.114.v) | copy-start | bytes 3366916
  69.9 20.8 %collective-permute-start.10 = (f32[1,137,128]{2,1,0:T(8,128)}, f32[1,137,128]{2,1,0:T(8,128)}, u32[]{:S(2)}, u32[]{:S(2)}) collective-permute-start(f32[1,137,128]{2,1,0:T(8,128)} %get-tuple-element.35), channel_id=1, source_target_pairs={{0,4},{4,8},{8,12},{1,5},{5,9},{9,13},{2,6},{6,10},{10,14},{3,7},{... | collective-permute-start | bytes 210440 | tf_op jit(solution)/shard_map/ppermute | solution.py:16
  75.1 15.6 %collective-permute-start.11 = (f32[1,137,128]{2,1,0:T(8,128)}, f32[1,137,128]{2,1,0:T(8,128)}, u32[]{:S(2)}, u32[]{:S(2)}) collective-permute-start(f32[1,137,128]{2,1,0:T(8,128)} %get-tuple-element.34), channel_id=1, source_target_pairs={{4,0},{8,4},{12,8},{5,1},{9,5},{13,9},{6,2},{10,6},{14,10},{7,3},{... | collective-permute-start | bytes 210440 | tf_op jit(solution)/shard_map/ppermute | solution.py:16
  78.6 7.6 %collective-permute-start.12 = (f32[16,137]{1,0:T(8,128)}, f32[16,137]{1,0:T(8,128)}, u32[]{:S(2)}, u32[]{:S(2)}) collective-permute-start(f32[16,137]{1,0:T(8,128)} %get-tuple-element.17), channel_id=1, source_target_pairs={{0,1},{1,2},{2,3},{4,5},{5,6},{6,7},{8,9},{9,10},{10,11},{12,13},{... | collective-permute-start | bytes 26312 | tf_op jit(solution)/shard_map/ppermute | solution.py:16
  83.3 5.2 %collective-permute-start.13 = (f32[16,137]{1,0:T(8,128)S(1)}, f32[16,137]{1,0:T(8,128)}, u32[]{:S(2)}, u32[]{:S(2)}) collective-permute-start(f32[16,137]{1,0:T(8,128)S(1)} %get-tuple-element.16), channel_id=1, source_target_pairs={{1,0},{2,1},{3,2},{5,4},{6,5},{7,6},{9,8},{10,9},{11,10},{13,12},{... | collective-permute-start | bytes 26312 | tf_op jit(solution)/shard_map/ppermute | solution.py:16
  101.5 94.1 %collective-permute-start.14 = (f32[137,16,128]{2,1,0:T(8,128)}, f32[137,16,128]{2,1,0:T(8,128)}, u32[]{:S(2)}, u32[]{:S(2)}) collective-permute-start(f32[137,16,128]{2,1,0:T(8,128)} %copy.132), channel_id=1, source_target_pairs={{0,16},{1,17},{2,18},{3,19},{4,20},{5,21},{6,22},{7,23},{8,24},{9,... | collective-permute-start | bytes 3366920 | tf_op jit(solution)/shard_map/ppermute | solution.py:16
  112.1 8.4 %copy-start.10 = (f32[16,137,128]{2,1,0:T(8,128)}, f32[16,137,128]{2,1,0:T(8,128)S(1)}, u32[]{:S(2)}) copy-start(f32[16,137,128]{2,1,0:T(8,128)S(1)} %shard_map.116.v) | copy-start | bytes 3366916
  112.8 18.2 %collective-permute-start.16 = (f32[1,137,128]{2,1,0:T(8,128)}, f32[1,137,128]{2,1,0:T(8,128)}, u32[]{:S(2)}, u32[]{:S(2)}) collective-permute-start(f32[1,137,128]{2,1,0:T(8,128)} %get-tuple-element.33), channel_id=1, source_target_pairs={{0,4},{4,8},{8,12},{1,5},{5,9},{9,13},{2,6},{6,10},{10,14},{3,7},{... | collective-permute-start | bytes 210440 | tf_op jit(solution)/shard_map/ppermute | solution.py:16
  117.7 13.3 %collective-permute-start.17 = (f32[1,137,128]{2,1,0:T(8,128)}, f32[1,137,128]{2,1,0:T(8,128)}, u32[]{:S(2)}, u32[]{:S(2)}) collective-permute-start(f32[1,137,128]{2,1,0:T(8,128)} %get-tuple-element.32), channel_id=1, source_target_pairs={{4,0},{8,4},{12,8},{5,1},{9,5},{13,9},{6,2},{10,6},{14,10},{7,3},{... | collective-permute-start | bytes 210440 | tf_op jit(solution)/shard_map/ppermute | solution.py:16
  120.5 4.6 %collective-permute-start.18 = (f32[16,137]{1,0:T(8,128)S(1)}, f32[16,137]{1,0:T(8,128)S(1)}, u32[]{:S(2)}, u32[]{:S(2)}) collective-permute-start(f32[16,137]{1,0:T(8,128)S(1)} %get-tuple-element.15), channel_id=1, source_target_pairs={{0,1},{1,2},{2,3},{4,5},{5,6},{6,7},{8,9},{9,10},{10,11},{12,13},{... | collective-permute-start | bytes 26312 | tf_op jit(solution)/shard_map/ppermute | solution.py:16
  123.8 5.0 %collective-permute-start.19 = (f32[16,137]{1,0:T(8,128)S(1)}, f32[16,137]{1,0:T(8,128)}, u32[]{:S(2)}, u32[]{:S(2)}) collective-permute-start(f32[16,137]{1,0:T(8,128)S(1)} %get-tuple-element.14), channel_id=1, source_target_pairs={{1,0},{2,1},{3,2},{5,4},{6,5},{7,6},{9,8},{10,9},{11,10},{13,12},{... | collective-permute-start | bytes 26312 | tf_op jit(solution)/shard_map/ppermute | solution.py:16
  139.6 8.7 %copy-start.8 = (f32[16,137,128]{2,1,0:T(8,128)}, f32[16,137,128]{2,1,0:T(8,128)S(1)}, u32[]{:S(2)}) copy-start(f32[16,137,128]{2,1,0:T(8,128)S(1)} %shard_map.117.v) | copy-start | bytes 3366916
  140.4 18.6 %collective-permute-start.20 = (f32[1,137,128]{2,1,0:T(8,128)}, f32[1,137,128]{2,1,0:T(8,128)}, u32[]{:S(2)}, u32[]{:S(2)}) collective-permute-start(f32[1,137,128]{2,1,0:T(8,128)} %get-tuple-element.31), channel_id=1, source_target_pairs={{0,4},{4,8},{8,12},{1,5},{5,9},{9,13},{2,6},{6,10},{10,14},{3,7},{... | collective-permute-start | bytes 210440 | tf_op jit(solution)/shard_map/ppermute | solution.py:16
  145.5 13.4 %collective-permute-start.21 = (f32[1,137,128]{2,1,0:T(8,128)}, f32[1,137,128]{2,1,0:T(8,128)}, u32[]{:S(2)}, u32[]{:S(2)}) collective-permute-start(f32[1,137,128]{2,1,0:T(8,128)} %get-tuple-element.30), channel_id=1, source_target_pairs={{4,0},{8,4},{12,8},{5,1},{9,5},{13,9},{6,2},{10,6},{14,10},{7,3},{... | collective-permute-start | bytes 210440 | tf_op jit(solution)/shard_map/ppermute | solution.py:16
  148.3 5.6 %collective-permute-start.22 = (f32[16,137]{1,0:T(8,128)S(1)}, f32[16,137]{1,0:T(8,128)S(1)}, u32[]{:S(2)}, u32[]{:S(2)}) collective-permute-start(f32[16,137]{1,0:T(8,128)S(1)} %get-tuple-element.13), channel_id=1, source_target_pairs={{0,1},{1,2},{2,3},{4,5},{5,6},{6,7},{8,9},{9,10},{10,11},{12,13},{... | collective-permute-start | bytes 26312 | tf_op jit(solution)/shard_map/ppermute | solution.py:16
  152.4 4.3 %collective-permute-start.23 = (f32[16,137]{1,0:T(8,128)S(1)}, f32[16,137]{1,0:T(8,128)}, u32[]{:S(2)}, u32[]{:S(2)}) collective-permute-start(f32[16,137]{1,0:T(8,128)S(1)} %get-tuple-element.12), channel_id=1, source_target_pairs={{1,0},{2,1},{3,2},{5,4},{6,5},{7,6},{9,8},{10,9},{11,10},{13,12},{... | collective-permute-start | bytes 26312 | tf_op jit(solution)/shard_map/ppermute | solution.py:16
  167.6 8.7 %copy-start.2 = (f32[16,137,128]{2,1,0:T(8,128)}, f32[16,137,128]{2,1,0:T(8,128)S(1)}, u32[]{:S(2)}) copy-start(f32[16,137,128]{2,1,0:T(8,128)S(1)} %shard_map.118.v) | copy-start | bytes 3366916
  168.3 18.8 %collective-permute-start.24 = (f32[1,137,128]{2,1,0:T(8,128)}, f32[1,137,128]{2,1,0:T(8,128)}, u32[]{:S(2)}, u32[]{:S(2)}) collective-permute-start(f32[1,137,128]{2,1,0:T(8,128)} %get-tuple-element.29), channel_id=1, source_target_pairs={{0,4},{4,8},{8,12},{1,5},{5,9},{9,13},{2,6},{6,10},{10,14},{3,7},{... | collective-permute-start | bytes 210440 | tf_op jit(solution)/shard_map/ppermute | solution.py:16
  173.5 13.6 %collective-permute-start.25 = (f32[1,137,128]{2,1,0:T(8,128)}, f32[1,137,128]{2,1,0:T(8,128)}, u32[]{:S(2)}, u32[]{:S(2)}) collective-permute-start(f32[1,137,128]{2,1,0:T(8,128)} %get-tuple-element.28), channel_id=1, source_target_pairs={{4,0},{8,4},{12,8},{5,1},{9,5},{13,9},{6,2},{10,6},{14,10},{7,3},{... | collective-permute-start | bytes 210440 | tf_op jit(solution)/shard_map/ppermute | solution.py:16
  176.3 5.4 %collective-permute-start.26 = (f32[16,137]{1,0:T(8,128)S(1)}, f32[16,137]{1,0:T(8,128)S(1)}, u32[]{:S(2)}, u32[]{:S(2)}) collective-permute-start(f32[16,137]{1,0:T(8,128)S(1)} %get-tuple-element.11), channel_id=1, source_target_pairs={{0,1},{1,2},{2,3},{4,5},{5,6},{6,7},{8,9},{9,10},{10,11},{12,13},{... | collective-permute-start | bytes 26312 | tf_op jit(solution)/shard_map/ppermute | solution.py:16
  180.3 4.5 %collective-permute-start.27 = (f32[16,137]{1,0:T(8,128)S(1)}, f32[16,137]{1,0:T(8,128)}, u32[]{:S(2)}, u32[]{:S(2)}) collective-permute-start(f32[16,137]{1,0:T(8,128)S(1)} %get-tuple-element.10), channel_id=1, source_target_pairs={{1,0},{2,1},{3,2},{5,4},{6,5},{7,6},{9,8},{10,9},{11,10},{13,12},{... | collective-permute-start | bytes 26312 | tf_op jit(solution)/shard_map/ppermute | solution.py:16
  192.7 2.9 %copy-start.40 = (f32[1,137,16,128]{3,2,1,0:T(8,128)S(1)}, f32[1,137,16,128]{3,2,1,0:T(8,128)}, u32[]{:S(2)}) copy-start(f32[1,137,16,128]{3,2,1,0:T(8,128)} %param.11) | copy-start | bytes 3366916
  192.7 2.9 %copy-start.41 = (f32[1,137,16,128]{3,2,1,0:T(8,128)S(1)}, f32[1,137,16,128]{3,2,1,0:T(8,128)}, u32[]{:S(2)}) copy-start(f32[1,137,16,128]{3,2,1,0:T(8,128)} %param.17) | copy-start | bytes 3366916
  192.7 2.9 %copy-start.42 = (f32[1,137,16,128]{3,2,1,0:T(8,128)S(1)}, f32[1,137,16,128]{3,2,1,0:T(8,128)}, u32[]{:S(2)}) copy-start(f32[1,137,16,128]{3,2,1,0:T(8,128)} %param.13) | copy-start | bytes 3366916
  192.7 2.9 %copy-start.43 = (f32[1,137,16,128]{3,2,1,0:T(8,128)S(1)}, f32[1,137,16,128]{3,2,1,0:T(8,128)}, u32[]{:S(2)}) copy-start(f32[1,137,16,128]{3,2,1,0:T(8,128)} %param.16) | copy-start | bytes 3366916
  192.7 3.0 %copy-start.44 = (f32[1,137,16,128]{3,2,1,0:T(8,128)S(1)}, f32[1,137,16,128]{3,2,1,0:T(8,128)}, u32[]{:S(2)}) copy-start(f32[1,137,16,128]{3,2,1,0:T(8,128)} %param.12) | copy-start | bytes 3366916
  195.5 28.4 %copy-start.39 = (f32[1,137,16,128]{3,2,1,0:T(8,128)S(1)}, f32[1,137,16,128]{3,2,1,0:T(8,128)}, u32[]{:S(2)}) copy-start(f32[1,137,16,128]{3,2,1,0:T(8,128)} %param.10) | copy-start | bytes 3366916
  201.3 3.3 %collective-permute-start.28 = (f32[]{:T(128)}, f32[]{:T(128)}, u32[]{:S(2)}, u32[]{:S(2)}) collective-permute-start(f32[]{:T(128)} %add.35), channel_id=1, source_target_pairs={{0,1},{1,0},{2,3},{3,2},{4,5},{5,4},{6,7},{7,6},{8,9},{9,8},{10,11... | collective-permute-start | bytes 20 | tf_op jit(solution)/shard_map/ppermute | solution.py:25
  205.3 3.6 %collective-permute-start.29 = (f32[]{:T(128)}, f32[]{:T(128)}, u32[]{:S(2)}, u32[]{:S(2)}) collective-permute-start(f32[]{:T(128)} %add.36), channel_id=1, source_target_pairs={{0,2},{1,3},{2,0},{3,1},{4,6},{5,7},{6,4},{7,5},{8,10},{9,11},{10,... | collective-permute-start | bytes 20 | tf_op jit(solution)/shard_map/ppermute | solution.py:25
  209.5 4.2 %collective-permute-start.30 = (f32[]{:T(128)}, f32[]{:T(128)}, u32[]{:S(2)}, u32[]{:S(2)}) collective-permute-start(f32[]{:T(128)} %add.37), channel_id=1, source_target_pairs={{0,4},{4,0},{8,12},{12,8},{1,5},{5,1},{9,13},{13,9},{2,6},{6,2},{1... | collective-permute-start | bytes 20 | tf_op jit(solution)/shard_map/ppermute | solution.py:25
  214.4 4.5 %collective-permute-start.31 = (f32[]{:T(128)}, f32[]{:T(128)}, u32[]{:S(2)}, u32[]{:S(2)}) collective-permute-start(f32[]{:T(128)} %add.38), channel_id=1, source_target_pairs={{0,8},{4,12},{8,0},{12,4},{1,9},{5,13},{9,1},{13,5},{2,10},{6,14},... | collective-permute-start | bytes 20 | tf_op jit(solution)/shard_map/ppermute | solution.py:25
  219.6 3.6 %collective-permute-start.32 = (f32[]{:T(128)}, f32[]{:T(128)}, u32[]{:S(2)}, u32[]{:S(2)}) collective-permute-start(f32[]{:T(128)} %add.39), channel_id=1, source_target_pairs={{0,16},{16,0},{1,17},{17,1},{2,18},{18,2},{3,19},{19,3},{4,20},{20... | collective-permute-start | bytes 20 | tf_op jit(solution)/shard_map/ppermute | solution.py:25
  (37 other events, 41.9 us)
where the time goes:
time: 232 us; the launch traced here: 229 us
  starting transfers between devices  96.9 us (42%)
  local copies, waits for them, and re-layouts  89.8 us (39%)
  Pallas kernels  21.5 us (9%)
  waiting for transfers between devices  8.19 us (4%)
  other arithmetic  6.23 us (3%)
  between operations  5.98 us (3%)
    ppermute x28, starting transfers between devices, shifted(): return lax.ppermute(block, axis, route)  83.1 us
    unnamed x110, local copies, waits for them, and re-layouts  43.7 us
    pallas_call x7, Pallas kernels, step(): pl.pallas_call(functools.partial(kernel, adjoint, stencil, mix), out_shap...  21.5 us
    ppermute x5, starting transfers between devices, summed(): lax.ppermute(value, axis, [(i, i ^ bit) for i in range(count)])  13.8 us
    broadcast_in_dim x6, local copies, waits for them, and re-layouts, rims(): y_low = shifted(state[:, :, -1], 'gy', 1)[:, :, None]  13.3 us
    broadcast_in_dim x6, local copies, waits for them, and re-layouts, rims(): y_high = shifted(state[:, :, 0], 'gy', -1)[:, :, None]  13.2 us
    slice x6, local copies, waits for them, and re-layouts, rims(): y_high = shifted(state[:, :, 0], 'gy', -1)[:, :, None]  9.52 us
    ppermute x5, waiting for transfers between devices, summed(): lax.ppermute(value, axis, [(i, i ^ bit) for i in range(count)])  5.4 us
  transfers between devices with their start and end apart: 33, of which 8 were waited for; matrix products, arithmetic and copies ran while one was open for 22% of the time, Pallas kernels for 9%

commit v1 on v0

v1 whole, which is shorter than its diff:
```python
import functools

import jax
import jax.numpy as jnp
from jax import lax
from jax.experimental import pallas as pl
from jax.experimental.pallas import tpu as pltpu
from jax.sharding import PartitionSpec as P

STEPS = 3
MESH = pl.DeviceIdType.MESH
FIELDS = 8


def split(block):
    high = block.astype(jnp.bfloat16)
    return high, (block - high.astype(jnp.float32)).astype(jnp.bfloat16)


def kernel(
    axes,
    increment, dual, forcing, gradient, courant_x, courant_y, error_var, obs_weight, spread_row, matrix,
    out_dual, out_incr, out_scale,
    fwd, adj, ax, by, by_low, inbox, end, end_in, y_low, y_high, y_b, s_low, s_high, s_b,
    dual_v, forcing_v, gradient_v, error_v, obs_v, spread, mat_v, spread_v, mat, mat_t, acc, part, parts,
    load_sem, small_sem, out_sem, u_send, u_recv, e_send, e_recv,
    x_send, x_recv, y_send, y_recv, c_send, c_recv, r_send, r_recv,
):
    windows, nx, ny = axes
    count = windows * nx * ny
    rows, levels, width = dual_v.shape
    pairs = rows // 2
    stack = mat.shape[0] // 2
    k, gx, gy = lax.axis_index("tm"), lax.axis_index("gx"), lax.axis_index("gy")
    me = (k * nx + gx) * ny + gy
    has_next, has_prev = k < windows - 1, k > 0
    x_first, x_last = gx == 0, gx == nx - 1
    y_first, y_last = gy == 0, gy == ny - 1
    lane = lax.broadcasted_iota(jnp.int32, (levels, width), 1)

    def remote(src, dst, send, recv, where):
        return pltpu.make_async_remote_copy(
            src_ref=src, dst_ref=dst, send_sem=send, recv_sem=recv, device_id=where, device_id_type=MESH
        )

    def loop(n, body, start=0):
        def step(i, carry):
            body(i)
            return carry

        lax.fori_loop(start, n, step, 0)

    homes = (
        (increment, lambda i: fwd.at[0, i + 1]),
        (courant_y, lambda i: by.at[i]),
        (courant_x, lambda i: ax.at[i + 1]),
        (dual, lambda i: dual_v.at[i]),
        (forcing, lambda i: forcing_v.at[i]),
        (gradient, lambda i: gradient_v.at[i]),
        (error_var, lambda i: error_v.at[i]),
        (obs_weight, lambda i: obs_v.at[i]),
    )

    def load(f, i):
        source, home = homes[f]
        return pltpu.make_async_copy(source.at[:, i, 0], home(i), load_sem.at[f, i])

    small = (
        pltpu.make_async_copy(spread_row, spread_v, small_sem.at[0]),
        pltpu.make_async_copy(matrix, mat_v, small_sem.at[1]),
    )
    for copy in small:
        copy.start()
    for f in range(FIELDS):
        loop(rows, lambda i, f=f: load(f, i).start())

    barrier = pltpu.get_barrier_semaphore()

    def coords(flat):
        return {"tm": flat // (nx * ny), "gx": (flat // ny) % nx, "gy": flat % ny}

    def greet(d):
        pl.semaphore_signal(barrier, inc=1, device_id=coords((me + d) % count), device_id_type=MESH)

    loop(count, greet, 1)

    for copy in small:
        copy.wait()
    spread[...] = jnp.swapaxes(jnp.broadcast_to(spread_v[...], (width, levels)), 0, 1)
    for source, home in ((mat_v[...], mat), (jnp.swapaxes(mat_v[...], 0, 1), mat_t)):
        high, low = split(source)
        home[0:levels, :] = high
        home[stack : stack + levels, :] = low
    acc[...] = jnp.zeros_like(acc)

    zero = jnp.zeros((levels, width), jnp.float32)

    @pl.when(x_first)
    def _():
        ax[0] = zero
        for s in range(STEPS):
            fwd[s, 0] = zero
            adj[s, 0] = zero

    @pl.when(x_last)
    def _():
        for s in range(STEPS):
            fwd[s, rows + 1] = zero
            adj[s, rows + 1] = zero

    @pl.when(y_first)
    def _():
        y_b[...] = zero
        for s in range(2 * STEPS):
            y_low[s] = zero

    @pl.when(y_last)
    def _():
        for s in range(2 * STEPS):
            y_high[s] = zero

    pl.semaphore_wait(barrier, count - 1)

    def order(t):
        return (t // 2) * (1 - 2 * (t % 2)) + (t % 2) * (pairs - 1)

    def dual_copy(i):
        return remote(dual.at[:, i, 0], inbox.at[i], u_send.at[i], u_recv.at[i], {"tm": k - 1})

    @pl.when(has_prev)
    def _():
        def send(t):
            p = order(t)
            dual_copy(2 * p).start()
            dual_copy(2 * p + 1).start()

        loop(pairs, send)

    def state(n):
        return fwd.at[n] if n < STEPS else adj.at[n - STEPS]

    def x_up(n):
        src = increment.at[:, rows - 1, 0] if n == 0 else state(n).at[rows]
        return remote(src, state(n).at[0], x_send.at[n, 0], x_recv.at[n, 0], {"gx": gx + 1})

    def x_down(n):
        src = increment.at[:, 0, 0] if n == 0 else state(n).at[1]
        return remote(src, state(n).at[rows + 1], x_send.at[n, 1], x_recv.at[n, 1], {"gx": gx - 1})

    def y_up(n):
        return remote(s_high.at[n], y_low.at[n], y_send.at[n, 0], y_recv.at[n, 0], {"gy": gy + 1})

    def y_down(n):
        return remote(s_low.at[n], y_high.at[n], y_send.at[n, 1], y_recv.at[n, 1], {"gy": gy - 1})

    def a_up():
        return remote(courant_x.at[:, rows - 1, 0], ax.at[0], c_send.at[0], c_recv.at[0], {"gx": gx + 1})

    def b_up():
        return remote(s_b, y_b, c_send.at[1], c_recv.at[1], {"gy": gy + 1})

    def start_x(n):
        pl.when(jnp.logical_not(x_last))(lambda: x_up(n).start())
        pl.when(jnp.logical_not(x_first))(lambda: x_down(n).start())

    def start_y(n):
        pl.when(jnp.logical_not(y_last))(lambda: y_up(n).start())
        pl.when(jnp.logical_not(y_first))(lambda: y_down(n).start())

    def wait_halo(n):
        pl.when(jnp.logical_not(x_first))(lambda: x_up(n).wait_recv())
        pl.when(jnp.logical_not(x_last))(lambda: x_down(n).wait_recv())
        pl.when(jnp.logical_not(y_first))(lambda: y_up(n).wait_recv())
        pl.when(jnp.logical_not(y_last))(lambda: y_down(n).wait_recv())

    def sent_halo(n):
        pl.when(jnp.logical_not(x_last))(lambda: x_up(n).wait_send())
        pl.when(jnp.logical_not(x_first))(lambda: x_down(n).wait_send())
        pl.when(jnp.logical_not(y_last))(lambda: y_up(n).wait_send())
        pl.when(jnp.logical_not(y_first))(lambda: y_down(n).wait_send())

    def pack(n, i, value):
        s_high[n] = jnp.where(lane == i, pltpu.roll(value, i + 1, 1), s_high[n])
        s_low[n] = jnp.where(lane == i, pltpu.roll(value, i, 1), s_low[n])

    def around(n, i):
        v = state(n)[i + 1]
        before, after = state(n)[i], state(n)[i + 2]
        left = jnp.where(lane == 0, pltpu.roll(y_low[n], (width - i) % width, 1), pltpu.roll(v, 1, 1))
        right = jnp.where(
            lane == width - 1, pltpu.roll(y_high[n], width - 1 - i, 1), pltpu.roll(v, width - 1, 1)
        )
        return v, before, after, left, right

    def forward_row(n, i):
        v, before, after, left, right = around(n, i)
        s = spread[...]
        flow = (1.0 - 4.0 * s - ax[i + 1] - by[i]) * v + ax[i] * before + by_low[i] * left
        return flow + s * (before + after + left + right)

    def adjoint_row(n, i):
        w, before, after, left, right = around(n, i)
        s = spread[...]
        a, b = ax[i + 1], by[i]
        flow = (1.0 - 4.0 * s - a - b) * w + a * after + b * right
        return flow + s * (before + after + left + right)

    def mixed(mats, first, second):
        high, low = split(jnp.concatenate([first, second], axis=1))
        dot = functools.partial(jnp.dot, preferred_element_type=jnp.float32)
        wide = dot(mats[...], high)
        result = dot(mats[0:levels, :], low) + wide[stack : stack + levels] + wide[0:levels]
        return result[:, :width], result[:, width:]

    def end_copy(i):
        return remote(end.at[i], end_in.at[i], e_send.at[i], e_recv.at[i], {"tm": k + 1})

    def advance(n, row, mats, last):
        def body(t):
            p = order(t)
            for i, value in zip((2 * p, 2 * p + 1), mixed(mats, row(n, 2 * p), row(n, 2 * p + 1))):
                if last:
                    end[i] = value
                else:
                    state(n + 1)[i + 1] = value
                    pack(n + 1, i, value)

        return body

    for f in (0, 1, 2):
        loop(rows, lambda i, f=f: load(f, i).wait())

    @pl.when(has_next)
    def _():
        start_x(0)
        pl.when(jnp.logical_not(x_last))(lambda: a_up().start())

        def pack_inputs(i):
            pack(0, i, fwd[0, i + 1])
            s_b[...] = jnp.where(lane == i, pltpu.roll(by[i], i + 1, 1), s_b[...])

        loop(rows, pack_inputs)
        start_y(0)
        pl.when(jnp.logical_not(y_last))(lambda: b_up().start())
        pl.when(jnp.logical_not(x_first))(lambda: a_up().wait_recv())
        pl.when(jnp.logical_not(y_first))(lambda: b_up().wait_recv())

        def lower(i):
            by_low[i] = jnp.where(
                lane == 0, pltpu.roll(y_b[...], (width - i) % width, 1), pltpu.roll(by[i], 1, 1)
            )

        loop(rows, lower)

        for n in range(STEPS):
            last = n == STEPS - 1
            body = advance(n, forward_row, mat, last)
            wait_halo(n)
            if not last:
                loop(2, body)
                start_x(n + 1)
                loop(pairs, body, 2)
                start_y(n + 1)
            else:
                def send(t):
                    p = order(t)
                    end_copy(2 * p).start()
                    end_copy(2 * p + 1).start()

                def both(t):
                    body(t)
                    pl.when(t > 0)(lambda: send(t - 1))

                loop(pairs, both)
                send(pairs - 1)

        def enter(t):
            p = order(t)
            dual_in = (2 * p, 2 * p + 1)
            for i in dual_in:
                dual_copy(i).wait_recv()
            for i, value in zip(dual_in, mixed(mat_t, inbox[2 * p], inbox[2 * p + 1])):
                adj[0, i + 1] = value
                pack(STEPS, i, value)

        loop(2, enter)
        start_x(STEPS)
        loop(pairs, enter, 2)
        start_y(STEPS)
        for n in range(STEPS, 2 * STEPS - 1):
            body = advance(n, adjoint_row, mat_t, False)
            wait_halo(n)
            loop(2, body)
            start_x(n + 1)
            loop(pairs, body, 2)
            start_y(n + 1)
        wait_halo(2 * STEPS - 1)

    for f in range(3, FIELDS):
        loop(rows, lambda i, f=f: load(f, i).wait())

    def result(ref, out, which, i):
        return pltpu.make_async_copy(ref.at[i], out.at[:, i, 0], out_sem.at[which, i])

    def residual_incr(i, back):
        value = gradient_v[i] - obs_v[i] * fwd[0, i + 1] - dual_v[i]
        if back:
            value = value + adjoint_row(2 * STEPS - 1, i)
        gradient_v[i] = value
        acc[...] += value * value

    def residual_dual(i, earlier):
        value = forcing_v[i] - error_v[i] * dual_v[i] - fwd[0, i + 1]
        if earlier:
            end_copy(i).wait_recv()
            value = value + end_in[i]
        forcing_v[i] = value
        acc[...] += value * value

    def send_out(ref, out, which):
        loop(rows, lambda i: result(ref, out, which, i).start())

    pl.when(has_next)(lambda: loop(rows, lambda i: residual_incr(i, True)))
    pl.when(jnp.logical_not(has_next))(lambda: loop(rows, lambda i: residual_incr(i, False)))
    send_out(gradient_v, out_incr, 1)

    @pl.when(has_prev)
    def _():
        def body(t):
            p = order(t)
            residual_dual(2 * p, True)
            residual_dual(2 * p + 1, True)

        loop(pairs, body)

    pl.when(jnp.logical_not(has_prev))(lambda: loop(rows, lambda i: residual_dual(i, False)))
    send_out(forcing_v, out_dual, 0)

    part[...] = jnp.sum(acc[...], axis=0, keepdims=True)
    parts[me] = part[...]

    def tell(d):
        other = (me + d) % count
        return remote(part, parts.at[me], r_send.at[d], r_recv.at[me], coords(other))

    def hear(d):
        other = (me + count - d) % count
        return remote(part, parts.at[other], r_send.at[d], r_recv.at[other], coords(other))

    loop(count, lambda d: tell(d).start(), 1)
    loop(count, lambda d: hear(d).wait_recv(), 1)
    total = jnp.sum(jnp.sum(parts[...], axis=0), axis=1, keepdims=True)
    cells = 2 * rows * levels * width * count
    root_mean = jnp.sqrt(total / cells + 1e-06)
    out_scale[...] = jnp.broadcast_to(jnp.minimum(1.0, 0.5 / root_mean), out_scale.shape)

    loop(count, lambda d: tell(d).wait_send(), 1)
    for ref, out, which in ((forcing_v, out_dual, 0), (gradient_v, out_incr, 1)):
        loop(rows, lambda i: result(ref, out, which, i).wait())
    pl.when(has_prev)(lambda: loop(rows, lambda i: dual_copy(i).wait_send()))

    @pl.when(has_next)
    def _():
        loop(rows, lambda i: end_copy(i).wait_send())
        pl.when(jnp.logical_not(x_last))(lambda: a_up().wait_send())
        pl.when(jnp.logical_not(y_last))(lambda: b_up().wait_send())
        for n in range(2 * STEPS):
            sent_halo(n)


def local(axes, increment, dual_state, forcing, gradient, courant_x, courant_y, error_var, obs_weight, diffusion, level_mix):
    levels, rows, width = increment.shape[1:]
    count = axes[0] * axes[1] * axes[2]
    stack = -(-levels // 16) * 16
    fields = [
        part.reshape(levels, rows, 1, width)
        for part in (increment, dual_state, forcing, gradient, courant_x, courant_y, error_var, obs_weight)
    ]
    slab = lambda *lead: pltpu.VMEM((*lead, levels, width), jnp.float32)
    dma = lambda *shape: pltpu.SemaphoreType.DMA(shape)
    scratch = [
        slab(STEPS, rows + 2), slab(STEPS, rows + 2), slab(rows + 1), slab(rows), slab(rows),
        slab(rows), slab(rows), slab(rows),
        slab(2 * STEPS), slab(2 * STEPS), slab(), slab(2 * STEPS), slab(2 * STEPS), slab(),
        slab(rows), slab(rows), slab(rows), slab(rows), slab(rows),
        slab(), pltpu.VMEM((levels, levels), jnp.float32), pltpu.VMEM((1, levels), jnp.float32),
        pltpu.VMEM((2 * stack, levels), jnp.bfloat16), pltpu.VMEM((2 * stack, levels), jnp.bfloat16),
        slab(), pltpu.VMEM((1, width), jnp.float32), pltpu.VMEM((count, 1, width), jnp.float32),
        dma(FIELDS, rows), dma(2), dma(2, rows), dma(rows), dma(rows), dma(rows), dma(rows),
        dma(2 * STEPS, 2), dma(2 * STEPS, 2), dma(2 * STEPS, 2), dma(2 * STEPS, 2), dma(2), dma(2),
        dma(count), dma(count),
    ]
    field = jax.ShapeDtypeStruct((levels, rows, 1, width), jnp.float32)
    anywhere = pl.BlockSpec(memory_space=pltpu.HBM)
    residual_dual, residual_incr, scale = pl.pallas_call(
        functools.partial(kernel, axes),
        out_shape=(field, field, jax.ShapeDtypeStruct((1, width), jnp.float32)),
        in_specs=[anywhere] * 10,
        out_specs=(anywhere, anywhere, pl.BlockSpec(memory_space=pltpu.VMEM)),
        scratch_shapes=scratch,
        compiler_params=pltpu.CompilerParams(
            collective_id=0, has_side_effects=True, vmem_limit_bytes=63 * 1024 * 1024
        ),
    )(*fields, diffusion[None, :], level_mix)
    scale = scale[0, 0]
    dual_next = dual_state + scale * residual_dual.reshape(dual_state.shape)
    increment_next = increment + scale * residual_incr.reshape(increment.shape)
    return dual_next, increment_next


def solution(mesh):
    spec = P("tm", None, "gx", "gy")
    axes = tuple(mesh.shape[name] for name in ("tm", "gx", "gy"))
    return jax.shard_map(
        functools.partial(local, axes),
        mesh=mesh,
        in_specs=(spec,) * FIELDS + (P(), P()),
        out_specs=(spec, spec),
        check_vma=False,
    )
```

time: 232 us -> 71 us (0.31); the launches traced: 229 us -> 70.8 us
  starting transfers between devices: 96.9 us -> 0 us
  local copies, waits for them, and re-layouts: 89.8 us -> 0.28 us
  Pallas kernels: 21.5 us -> 65.1 us
  waiting for transfers between devices: 8.19 us -> 0 us
  between operations: 5.98 us -> 0.67 us
    ppermute x33 -> x0, starting transfers between devices: 96.9 us -> none  [the longest x28 83.1 us: shifted(): return lax.ppermute(block, axis, route)]
    pallas_call x7 -> x1, Pallas kernels: 21.5 us -> 65.1 us  [local(): pl.pallas_call(functools.partial(kernel, axes), out_shape=(field, field,...]
    unnamed x110 -> x4, local copies, waits for them, and re-layouts: 43.7 us -> 0.28 us
    broadcast_in_dim x14 -> x0, local copies, waits for them, and re-layouts: 27.7 us -> none  [the longest x6 13.3 us: rims(): y_low = shifted(state[:, :, -1], 'gy', 1)[:, :, None]]
    slice x14 -> x0, local copies, waits for them, and re-layouts: 15.4 us -> none  [the longest x6 9.52 us: rims(): y_high = shifted(state[:, :, 0], 'gy', -1)[:, :, None]]
    ppermute x33 -> x0, waiting for transfers between devices: 8.19 us -> none  [the longest x5 5.4 us: summed(): lax.ppermute(value, axis, [(i, i ^ bit) for i in range(count)])]
    reduce_sum x1 -> x0, other arithmetic: 4.22 us -> none  [local(): jnp.sum(residual_incr * residual_incr)]
    mul x0 -> x1, other arithmetic: none -> 2.46 us  [local(): increment_next = increment + scale * residual_incr.reshape(increment.shape)]
  transfers between devices with their start and end apart: 33 -> 0, of which waited for: 8 -> 0; matrix products, arithmetic and copies ran while one was open for 22% -> 0% of each run, Pallas kernels for 9% -> 0%
where the time goes in v1:
time: 71 us; the launch traced here: 70.8 us
  Pallas kernels  65.1 us (92%)
  other arithmetic  4.8 us (7%)
    pallas_call x1, Pallas kernels, local(): pl.pallas_call(functools.partial(kernel, axes), out_shape=(field, field,...  65.1 us
    mul x1, other arithmetic, local(): increment_next = increment + scale * residual_incr.reshape(increment.shape)  2.46 us

profile of v1, /device:TPU:0, one launch (start us, length us, event | category | flops | bytes accessed | tf_op | source)
XLA Modules:
  0.0 70.8 jit_solution(11735326708368496863)
XLA Ops:
  0.6 65.1 %shard_map.113 = (f32[137,16,1,128]{3,2,1,0:T(1,128)}, f32[137,16,1,128]{3,2,1,0:T(1,128)}, f32[1,128]{1,0:T(1,128)}) custom-call(f32[137,16,1,128]{3,2,1,0:T(1,128)} %bitcast.20, f32[137,16,1,128]{3,2,1,0:T(1,128)} %bitcast.19, f32[137,16,1,128]{3,2,1,0:T(1,128)} %bitcast.23, f32[137,16,1,128]{3,2,1,0:T(1,128)} %bitcast.24, f32[137,16,1,128]{3,2,1,0:T(1,128)} %bitcast.25, ...), custom_call_target="tpu_custom_call" | custom-call | tf_op jit(solution)/shard_map/pallas_call | solution.py:395
  65.7 0.0 copy-start
  65.7 2.5 %broadcast_multiply_fusion = (f32[137,2,8,128]{3,2,1,0:T(8,128)S(1)}, f32[137,2,8,128]{3,2,1,0:T(8,128)S(1)}) fusion(f32[137,2,8,128]{3,2,1,0:T(8,128)} %bitcast.22, f32[]{:T(128)} %bitcast.30, f32[137,2,8,128]{3,2,1,0:T(8,128)} %bitcast.21), kind=kLoop, calls=%fused_computation | loop fusion | flops 561152 | bytes 4489220 | tf_op jit(solution)/shard_map/mul | solution.py:407
  68.2 0.0 copy-done
  68.2 0.0 copy-start.1
  68.2 1.2 %add.6 = f32[1,137,16,128]{3,2,1,0:T(8,128)} add(f32[1,137,16,128]{3,2,1,0:T(8,128)S(1)} %copy-done, f32[1,137,16,128]{3,2,1,0:T(8,128)S(1)} %bitcast.18) | non-fusion elementwise | flops 280576 | bytes 3366912 | tf_op jit(solution)/shard_map/add | solution.py:406
  69.4 0.3 copy-done.1
  69.7 1.1 %add.7 = f32[1,137,16,128]{3,2,1,0:T(8,128)} add(f32[1,137,16,128]{3,2,1,0:T(8,128)S(1)} %copy-done.1, f32[1,137,16,128]{3,2,1,0:T(8,128)S(1)} %bitcast.17) | non-fusion elementwise | flops 280576 | bytes 3366912 | tf_op jit(solution)/shard_map/add | solution.py:407
Async XLA Ops:
  65.7 2.5 %copy-start = (f32[1,137,16,128]{3,2,1,0:T(8,128)S(1)}, f32[1,137,16,128]{3,2,1,0:T(8,128)}, u32[]{:S(2)}) copy-start(f32[1,137,16,128]{3,2,1,0:T(8,128)} %param.11) | copy-start | bytes 3366916
  68.2 1.5 %copy-start.1 = (f32[1,137,16,128]{3,2,1,0:T(8,128)S(1)}, f32[1,137,16,128]{3,2,1,0:T(8,128)}, u32[]{:S(2)}) copy-start(f32[1,137,16,128]{3,2,1,0:T(8,128)} %param.10) | copy-start | bytes 3366916

commit v2 on v1

v2 whole, which is shorter than its diff:
```python
import functools

import jax
import jax.numpy as jnp
from jax import lax
from jax.experimental import pallas as pl
from jax.experimental.pallas import tpu as pltpu
from jax.sharding import PartitionSpec as P

STEPS = 3
MESH = pl.DeviceIdType.MESH
FIELDS = 8
RIM = STEPS
GROUP = 2 * RIM


def split(block):
    high = block.astype(jnp.bfloat16)
    return high, (block - high.astype(jnp.float32)).astype(jnp.bfloat16)


def kernel(
    axes,
    increment, dual, forcing, gradient, courant_x, courant_y, error_var, obs_weight, spread_row, matrix,
    out_dual, out_incr, out_scale,
    v0, v1, v2, w0, w1, w2, ax, by, by_low, inbox, end, end_in,
    q_own, q_left, q_right, outside, q_dual, out_send, x_msg, x_msg_up, x_msg_down,
    pv, pu, pw, pa, pb,
    dual_v, forcing_v, gradient_v, error_v, obs_v, spread, mat_v, spread_v, mat, mat_t, acc, part, parts,
    load_sem, small_sem, out_sem, u_send, u_recv, e_send, e_recv, o_sem,
    x_send, x_recv, c_send, c_recv, q_send, q_recv, m_send, m_recv, r_send, r_recv, met,
):
    windows, nx, ny = axes
    count = windows * nx * ny
    rows, levels, width = dual_v.shape
    pairs = rows // 2
    quads = pairs // 2
    stack = mat.shape[0] // 2
    k, gx, gy = lax.axis_index("tm"), lax.axis_index("gx"), lax.axis_index("gy")
    me = (k * nx + gx) * ny + gy
    has_next, has_prev = k < windows - 1, k > 0
    not_ = jnp.logical_not
    x_first, x_last = gx == 0, gx == nx - 1
    y_first, y_last = gy == 0, gy == ny - 1
    lane = lax.broadcasted_iota(jnp.int32, (levels, width), 1)
    place = lane // GROUP - 2
    column = lane - (lane // GROUP) * GROUP
    near = column < RIM

    def remote(src, dst, send, recv, where):
        return pltpu.make_async_remote_copy(
            src_ref=src, dst_ref=dst, send_sem=send, recv_sem=recv, device_id=where, device_id_type=MESH
        )

    def loop(n, body, start=0):
        def step(i, carry):
            body(i)
            return carry

        lax.fori_loop(start, n, step, 0)

    homes = (
        (increment, lambda i: v0.at[i + 1]),
        (courant_y, lambda i: by.at[i]),
        (courant_x, lambda i: ax.at[i + 1]),
        (dual, lambda i: dual_v.at[i]),
        (forcing, lambda i: forcing_v.at[i]),
        (gradient, lambda i: gradient_v.at[i]),
        (error_var, lambda i: error_v.at[i]),
        (obs_weight, lambda i: obs_v.at[i]),
    )

    def load(f, i):
        source, home = homes[f]
        return pltpu.make_async_copy(source.at[:, i, 0], home(i), load_sem.at[f, i])

    def loaded(*which):
        for f in which:
            loop(rows, lambda i, f=f: load(f, i).wait())

    barrier = pltpu.get_barrier_semaphore()
    lines = (("tm", k, windows), ("gx", gx, nx), ("gy", gy, ny))

    def greet(semaphore, line):
        name, mine, size = line
        for d in range(1, size):
            other = lax.rem(mine + d, size)
            pl.semaphore_signal(semaphore, inc=1, device_id={name: other}, device_id_type=MESH)

    for line in lines:
        greet(barrier, line)

    small = (
        pltpu.make_async_copy(spread_row, spread_v, small_sem.at[0]),
        pltpu.make_async_copy(matrix, mat_v, small_sem.at[1]),
    )
    for copy in small:
        copy.start()
    for f in range(FIELDS):
        loop(rows, lambda i, f=f: load(f, i).start())

    for copy in small:
        copy.wait()
    spread[...] = jnp.swapaxes(jnp.broadcast_to(spread_v[...], (width, levels)), 0, 1)
    for source, home in ((mat_v[...], mat), (jnp.swapaxes(mat_v[...], 0, 1), mat_t)):
        high, low = split(source)
        home[0:levels, :] = high
        home[stack : stack + levels, :] = low
    acc[...] = jnp.zeros_like(acc)
    zero = jnp.zeros((levels, width), jnp.float32)

    @pl.when(x_first)
    def _():
        ax[0] = zero
        for state in (v0, v1, v2, w0, w1, w2):
            state[0] = zero

    @pl.when(x_last)
    def _():
        for state in (v0, v1, v2, w0, w1, w2):
            state[rows + 1] = zero

    pl.semaphore_wait(barrier, windows + nx + ny - 3)

    def quad_rows(q):
        low, high = quads - 1 - q, quads + q
        return (2 * low, 2 * low + 1, 2 * high, 2 * high + 1)

    def dual_copy(i):
        return remote(dual.at[:, i, 0], inbox.at[i], u_send.at[i], u_recv.at[i], {"tm": k - 1})

    def end_copy(i):
        return remote(end.at[i], end_in.at[i], e_send.at[i], e_recv.at[i], {"tm": k + 1})

    def outside_copy():
        return remote(out_send, outside, o_sem.at[0], o_sem.at[1], {"tm": k - 1})

    def send_quad(copy, q):
        for i in quad_rows(q):
            copy(i).start()

    chain = ((v0, v1, v2), (w0, w1, w2))

    def x_up(c, n):
        state = chain[c][n]
        src = increment.at[:, rows - 1, 0] if (c, n) == (0, 0) else state.at[rows]
        return remote(src, state.at[0], x_send.at[c, n, 0], x_recv.at[c, n, 0], {"gx": gx + 1})

    def x_down(c, n):
        state = chain[c][n]
        src = increment.at[:, 0, 0] if (c, n) == (0, 0) else state.at[1]
        return remote(src, state.at[rows + 1], x_send.at[c, n, 1], x_recv.at[c, n, 1], {"gx": gx - 1})

    def a_up():
        return remote(courant_x.at[:, rows - 1, 0], ax.at[0], c_send, c_recv, {"gx": gx + 1})

    def m_up(n):
        return remote(x_msg.at[n, 0], x_msg_up.at[n], m_send.at[n, 0], m_recv.at[n, 0], {"gx": gx + 1})

    def m_down(n):
        return remote(x_msg.at[n, 1], x_msg_down.at[n], m_send.at[n, 1], m_recv.at[n, 1], {"gx": gx - 1})

    def q_up(n):
        return remote(q_own.at[n], q_left.at[n], q_send.at[n, 0], q_recv.at[n, 0], {"gy": gy + 1})

    def q_down(n):
        return remote(q_own.at[n], q_right.at[n], q_send.at[n, 1], q_recv.at[n, 1], {"gy": gy - 1})

    def start_both(up, down, first, last):
        pl.when(not_(last))(lambda: up.start())
        pl.when(not_(first))(lambda: down.start())

    def heard_both(up, down, first, last):
        pl.when(not_(first))(lambda: up.wait_recv())
        pl.when(not_(last))(lambda: down.wait_recv())

    def sent_both(up, down, first, last):
        pl.when(not_(last))(lambda: up.wait_send())
        pl.when(not_(first))(lambda: down.wait_send())

    def x_start(c, n):
        start_both(x_up(c, n), x_down(c, n), x_first, x_last)

    def x_heard(c, n):
        heard_both(x_up(c, n), x_down(c, n), x_first, x_last)

    def turn(i):
        return GROUP * (i + 2) + RIM

    def pack_into(ref, index, i, value):
        ref[index] = jnp.where(place == i, pltpu.roll(value, turn(i) % width, 1), ref[index])

    inside_x = ((place >= 0) | not_(x_first)) & ((place < rows) | not_(x_last)) & (place < rows + 2)
    own_rows = (place >= 0) & (place < rows)
    inside = (
        inside_x & (not_(near) | not_(y_first)),
        inside_x & (near | not_(y_last)),
    )

    def assemble(target, index, own, left, right):
        target[index, 0] = jnp.where(inside[0] & own_rows, jnp.where(near, left, own), 0.0)
        target[index, 1] = jnp.where(inside[1] & own_rows, jnp.where(near, own, right), 0.0)

    def write_message(n, blocks):
        up, down = zero, zero
        for b, block in enumerate(blocks):
            mine = lane // (2 * GROUP) == b
            up = jnp.where(mine, pltpu.roll(block, (2 * GROUP * b - GROUP * rows) % width, 1), up)
            down = jnp.where(mine, pltpu.roll(block, (2 * GROUP * b - 2 * GROUP) % width, 1), down)
        x_msg[n, 0] = up
        x_msg[n, 1] = down
        start_both(m_up(n), m_down(n), x_first, x_last)

    def read_message(n, refs):
        heard_both(m_up(n), m_down(n), x_first, x_last)
        for b, (ref, index, side) in enumerate(refs):
            low = pltpu.roll(x_msg_up[n], (-2 * GROUP * b) % width, 1)
            high = pltpu.roll(x_msg_down[n], (GROUP * (rows + 2) - 2 * GROUP * b) % width, 1)
            value = jnp.where(place < 0, low, jnp.where(place >= rows, high, ref[index, side]))
            ref[index, side] = jnp.where(inside[side], value, 0.0)

    def mixed(mats, blocks):
        high, low = split(jnp.concatenate(blocks, axis=1))
        dot = functools.partial(jnp.dot, preferred_element_type=jnp.float32)
        wide = dot(mats[...], high)
        result = dot(mats[0:levels, :], low) + wide[stack : stack + levels] + wide[0:levels]
        return [result[:, j * width : (j + 1) * width] for j in range(len(blocks))]

    def sides(block, left_rim, right_rim, i):
        back = (2 * width - turn(i)) % width
        left = pltpu.roll(jnp.where(lane == width - 1, pltpu.roll(left_rim, back, 1), block), 1, 1)
        right = pltpu.roll(jnp.where(lane == 0, pltpu.roll(right_rim, back, 1), block), width - 1, 1)
        return left, right

    def forward_row(state, rim, i):
        v, before, after = state[i + 1], state[i], state[i + 2]
        left, right = sides(v, rim[0], rim[1], i)
        s = spread[...]
        flow = (1.0 - 4.0 * s - ax[i + 1] - by[i]) * v + ax[i] * before + by_low[i] * left
        return flow + s * (before + after + left + right)

    def adjoint_row(state, rim, i):
        w, before, after = state[i + 1], state[i], state[i + 2]
        left, right = sides(w, rim[0], rim[1], i)
        s = spread[...]
        a, b = ax[i + 1], by[i]
        flow = (1.0 - 4.0 * s - a - b) * w + a * after + b * right
        return flow + s * (before + after + left + right)

    def rim_parts(block):
        return (
            pltpu.roll(block, GROUP, 1), pltpu.roll(block, width - GROUP, 1),
            pltpu.roll(block, 1, 1), pltpu.roll(block, width - 1, 1),
        )

    def forward_rim(block, side):
        before, after, left, right = rim_parts(block)
        s, a, b = spread[...], pa[0, side], pb[0, side]
        flow = (1.0 - 4.0 * s - a - b) * block
        flow = flow + pltpu.roll(a, GROUP, 1) * before + pltpu.roll(b, 1, 1) * left
        return jnp.where(inside[side], flow + s * (before + after + left + right), 0.0)

    def adjoint_rim(block, side):
        before, after, left, right = rim_parts(block)
        s, a, b = spread[...], pa[0, side], pb[0, side]
        flow = (1.0 - 4.0 * s - a - b) * block + a * after + b * right
        return jnp.where(inside[side], flow + s * (before + after + left + right), 0.0)

    def advance_rim(ref, n, rule, mats):
        both = mixed(mats, [rule(ref[n, 0], 0), rule(ref[n, 1], 1)])
        ref[n + 1, 0], ref[n + 1, 1] = both

    def forward_quad(n, q):
        which = quad_rows(q)
        values = mixed(mat, [forward_row(chain[0][n], (pv[n, 0], pv[n, 1]), i) for i in which])
        for i, value in zip(which, values):
            if n == STEPS - 1:
                end[i] = value
            else:
                chain[0][n + 1][i + 1] = value

    def adjoint_quad(n, q):
        which = quad_rows(q)
        values = mixed(mat_t, [adjoint_row(chain[1][n], (pw[n, 0], pw[n, 1]), i) for i in which])
        for i, value in zip(which, values):
            chain[1][n + 1][i + 1] = value

    def enter(q):
        which = quad_rows(q)
        for i in which:
            dual_copy(i).wait_recv()
        values = mixed(mat_t, [inbox[i] for i in which])
        for i, value in zip(which, values):
            w0[i + 1] = value
        for i in which:
            pack_into(q_dual, 0, i, inbox[i])

    def enter_rim():
        own, far = q_dual[0], outside[...]
        assemble(pu, 0, own, far, far)

    def result(ref, out, which, i):
        return pltpu.make_async_copy(ref.at[i], out.at[:, i, 0], out_sem.at[which, i])

    def square(value):
        acc[...] += value * value

    def finish_dual(i, earlier):
        value = forcing_v[i]
        if earlier:
            end_copy(i).wait_recv()
            value = value + end_in[i]
            forcing_v[i] = value
        square(value)

    def early_residuals(i):
        d, v = dual_v[i], v0[i + 1]
        forcing_v[i] = forcing_v[i] - error_v[i] * d - v
        gradient_v[i] = gradient_v[i] - obs_v[i] * v - d

    @pl.when(has_prev)
    def _():
        send_quad(dual_copy, quads - 1)
        loaded(3)
        loop(rows, lambda i: pack_into(q_own, 3, i, dual_v[i]))
        start_both(q_up(3), q_down(3), y_first, y_last)
        heard_both(q_up(3), q_down(3), y_first, y_last)
        out_send[...] = jnp.where(near, q_left[3], q_right[3])
        send_quad(dual_copy, quads - 2)
        outside_copy().start()
        loop(quads - 2, lambda t: send_quad(dual_copy, quads - 3 - t))

    @pl.when(has_next)
    def _():
        x_start(0, 0)
        pl.when(not_(x_last))(lambda: a_up().start())
        for n, (f, value) in enumerate(
            ((0, lambda i: v0[i + 1]), (1, lambda i: by[i]), (2, lambda i: ax[i + 1]))
        ):
            loaded(f)
            loop(rows, lambda i, n=n, value=value: pack_into(q_own, n, i, value(i)))
            start_both(q_up(n), q_down(n), y_first, y_last)

    pl.when(not_(has_next))(lambda: loaded(0, 1, 2))
    for line, semaphore in ((lines[1], met.at[0]),):
        greet(semaphore, line)

    @pl.when(has_next)
    def _():
        for n, ref in enumerate((pv, pb, pa)):
            heard_both(q_up(n), q_down(n), y_first, y_last)
            assemble(ref, 0, q_own[n], q_left[n], q_right[n])
        write_message(0, [ref[0, side] for ref in (pv, pb, pa) for side in (0, 1)])

        def lower(i):
            back = (2 * width - turn(i)) % width
            by_low[i] = pltpu.roll(jnp.where(lane == width - 1, pltpu.roll(pb[0, 0], back, 1), by[i]), 1, 1)

        loop(rows, lower)
        loop(quads - 1, lambda q: forward_quad(0, q))
        x_heard(0, 0)
        pl.when(not_(x_first))(lambda: a_up().wait_recv())
        forward_quad(0, quads - 1)
        x_start(0, 1)
        advance_rim(pv, 0, forward_rim, mat)
        loop(quads - 1, lambda q: forward_quad(1, q))
        advance_rim(pv, 1, forward_rim, mat)

        def early_end(q):
            forward_quad(2, q)
            send_quad(end_copy, q)

        loop(quads - 2, early_end)

        read_message(0, [(ref, 0, side) for ref in (pv, pb, pa) for side in (0, 1)])
        advance_rim(pv, 0, forward_rim, mat)
        x_heard(0, 1)
        forward_quad(1, quads - 1)
        x_start(0, 2)
        advance_rim(pv, 1, forward_rim, mat)
        early_end(quads - 2)

    for f in range(3, FIELDS):
        if f == 3:
            pl.when(not_(has_prev))(lambda: loaded(3))
        else:
            loaded(f)
    loop(rows, early_residuals)

    @pl.when(not_(has_prev))
    def _():
        loop(rows, lambda i: finish_dual(i, False))
        loop(rows, lambda i: result(forcing_v, out_dual, 0, i).start())

    pl.semaphore_wait(met.at[0], nx - 1)
    greet(met.at[1], lines[0])

    @pl.when(has_next)
    def _():
        enter(quads - 1)
        x_start(1, 0)
        outside_copy().wait_recv()
        enter_rim()
        write_message(1, [pu[0, 0], pu[0, 1]])
        x_heard(0, 2)
        forward_quad(2, quads - 1)
        send_quad(end_copy, quads - 1)

        def rim_start():
            enter_rim_full()
            pw[0, 0], pw[0, 1] = mixed(mat_t, [pu[0, 0], pu[0, 1]])

        def enter_rim_full():
            own, far = q_dual[0], outside[...]
            for side, (left, right) in enumerate(((far, own), (own, far))):
                value = jnp.where(near, left, right)
                low = pltpu.roll(x_msg_up[1], (-2 * GROUP * side) % width, 1)
                high = pltpu.roll(x_msg_down[1], (GROUP * (rows + 2) - 2 * GROUP * side) % width, 1)
                value = jnp.where(place < 0, low, jnp.where(place >= rows, high, value))
                pu[0, side] = jnp.where(inside[side], value, 0.0)

        loop(quads - 1, lambda t: enter(quads - 2 - t))
        heard_both(m_up(1), m_down(1), x_first, x_last)
        rim_start()
        x_heard(1, 0)
        adjoint_quad(0, quads - 1)
        x_start(1, 1)
        loop(quads - 1, lambda t: adjoint_quad(0, t))
        advance_rim(pw, 0, adjoint_rim, mat_t)
        loop(quads - 1, lambda t: adjoint_quad(1, t))
        x_heard(1, 1)
        adjoint_quad(1, quads - 1)
        x_start(1, 2)
        advance_rim(pw, 1, adjoint_rim, mat_t)

        def finish_incr(q):
            for i in quad_rows(q):
                value = gradient_v[i] + adjoint_row(w2, (pw[2, 0], pw[2, 1]), i)
                gradient_v[i] = value
                square(value)

        loop(quads - 1, finish_incr)
        x_heard(1, 2)
        finish_incr(quads - 1)

    pl.when(not_(has_next))(lambda: loop(rows, lambda i: square(gradient_v[i])))
    loop(rows, lambda i: result(gradient_v, out_incr, 1, i).start())

    @pl.when(has_prev)
    def _():
        def body(q):
            for i in quad_rows(q):
                finish_dual(i, True)
            for i in quad_rows(q):
                result(forcing_v, out_dual, 0, i).start()

        loop(quads, body)

    pl.semaphore_wait(met.at[1], windows - 1)
    part[...] = jnp.sum(acc[...], axis=0, keepdims=True)
    parts[me] = part[...]

    def coords(flat):
        return {"tm": flat // (nx * ny), "gx": (flat // ny) % nx, "gy": flat % ny}

    def tell(d):
        other = (me + d) % count
        return remote(part, parts.at[me], r_send.at[d], r_recv.at[me], coords(other))

    def hear(d):
        other = (me + count - d) % count
        return remote(part, parts.at[other], r_send.at[d], r_recv.at[other], coords(other))

    loop(count, lambda d: tell(d).start(), 1)

    pl.when(has_prev)(lambda: loop(rows, lambda i: dual_copy(i).wait_send()))

    @pl.when(has_prev)
    def _():
        outside_copy().wait_send()
        sent_both(q_up(3), q_down(3), y_first, y_last)

    @pl.when(has_next)
    def _():
        loop(rows, lambda i: end_copy(i).wait_send())
        pl.when(not_(x_last))(lambda: a_up().wait_send())
        for n in range(STEPS):
            sent_both(x_up(0, n), x_down(0, n), x_first, x_last)
            sent_both(x_up(1, n), x_down(1, n), x_first, x_last)
            sent_both(q_up(n), q_down(n), y_first, y_last)
        for n in range(2):
            sent_both(m_up(n), m_down(n), x_first, x_last)

    for ref, out, which in ((forcing_v, out_dual, 0), (gradient_v, out_incr, 1)):
        loop(rows, lambda i: result(ref, out, which, i).wait())
    loop(count, lambda d: hear(d).wait_recv(), 1)
    total = jnp.sum(jnp.sum(parts[...], axis=0), axis=1, keepdims=True)
    cells = 2 * rows * levels * width * count
    root_mean = jnp.sqrt(total / cells + 1e-06)
    out_scale[...] = jnp.broadcast_to(jnp.minimum(1.0, 0.5 / root_mean), out_scale.shape)
    loop(count, lambda d: tell(d).wait_send(), 1)


def update(scale, dual, increment, residual_dual, residual_incr, dual_next, increment_next):
    dual_next[...] = dual[...] + scale[...] * residual_dual[...]
    increment_next[...] = increment[...] + scale[...] * residual_incr[...]


def local(axes, increment, dual_state, forcing, gradient, courant_x, courant_y, error_var, obs_weight, diffusion, level_mix):
    levels, rows, width = increment.shape[1:]
    count = axes[0] * axes[1] * axes[2]
    stack = -(-levels // 16) * 16
    assert rows % 4 == 0 and GROUP * (rows + 4) <= width
    fields = [
        part.reshape(levels, rows, 1, width)
        for part in (increment, dual_state, forcing, gradient, courant_x, courant_y, error_var, obs_weight)
    ]
    slab = lambda *lead: pltpu.VMEM((*lead, levels, width), jnp.float32)
    dma = lambda *shape: pltpu.SemaphoreType.DMA(shape)
    one = pltpu.SemaphoreType.DMA
    scratch = [
        *[slab(rows + 2)] * 6, slab(rows + 1), slab(rows), slab(rows), slab(rows), slab(rows), slab(rows),
        slab(4), slab(4), slab(4), slab(), slab(1), slab(), slab(2, 2), slab(2), slab(2),
        slab(3, 2), slab(1, 2), slab(3, 2), slab(1, 2), slab(1, 2),
        slab(rows), slab(rows), slab(rows), slab(rows), slab(rows),
        slab(), pltpu.VMEM((levels, levels), jnp.float32), pltpu.VMEM((1, levels), jnp.float32),
        pltpu.VMEM((2 * stack, levels), jnp.bfloat16), pltpu.VMEM((2 * stack, levels), jnp.bfloat16),
        slab(), pltpu.VMEM((1, width), jnp.float32), pltpu.VMEM((count, 1, width), jnp.float32),
        dma(FIELDS, rows), dma(2), dma(2, rows), dma(rows), dma(rows), dma(rows), dma(rows), dma(2),
        dma(2, STEPS, 2), dma(2, STEPS, 2), one, one, dma(4, 2), dma(4, 2), dma(2, 2), dma(2, 2),
        dma(count), dma(count), pltpu.SemaphoreType.REGULAR((2,)),
    ]
    field = jax.ShapeDtypeStruct((levels, rows, 1, width), jnp.float32)
    anywhere = pl.BlockSpec(memory_space=pltpu.HBM)
    residual_dual, residual_incr, scale = pl.pallas_call(
        functools.partial(kernel, axes),
        out_shape=(field, field, jax.ShapeDtypeStruct((1, width), jnp.float32)),
        in_specs=[anywhere] * 10,
        out_specs=(anywhere, anywhere, pl.BlockSpec(memory_space=pltpu.VMEM)),
        scratch_shapes=scratch,
        compiler_params=pltpu.CompilerParams(
            collective_id=0, has_side_effects=True, vmem_limit_bytes=63 * 1024 * 1024
        ),
    )(*fields, diffusion[None, :], level_mix)
    flat = lambda part: part.reshape(levels, rows, width)
    chunk = -(-levels // 4)
    block = pl.BlockSpec((chunk, rows, width), lambda i: (i, 0, 0))
    whole = jax.ShapeDtypeStruct((levels, rows, width), jnp.float32)
    results = pl.pallas_call(
        update,
        grid=(4,),
        out_shape=(whole, whole),
        in_specs=[pl.BlockSpec((1, 1, width), lambda i: (0, 0, 0))] + [block] * 4,
        out_specs=(block, block),
    )(scale.reshape(1, 1, width), *map(flat, (dual_state, increment, residual_dual, residual_incr)))
    return tuple(part.reshape(increment.shape) for part in results)


def solution(mesh):
    spec = P("tm", None, "gx", "gy")
    axes = tuple(mesh.shape[name] for name in ("tm", "gx", "gy"))
    return jax.shard_map(
        functools.partial(local, axes),
        mesh=mesh,
        in_specs=(spec,) * FIELDS + (P(), P()),
        out_specs=(spec, spec),
        check_vma=False,
    )
```

time: 71 us -> 60 us (0.85)
  Pallas kernels: 65.1 us -> 59.2 us
  other arithmetic: 4.8 us -> 0 us
    pallas_call x1, Pallas kernels: 65.1 us -> 55 us  [local(): pl.pallas_call(functools.partial(kernel, axes), out_shape=(field, field,...]
    pallas_call x0 -> x1, Pallas kernels: none -> 4.22 us  [local(): pl.pallas_call(update, grid=(4,), out_shape=(whole, whole), in_specs=[pl....]
    mul x1 -> x0, other arithmetic: 2.46 us -> none  [local(): increment_next = increment + scale * residual_incr.reshape(increment.shape)]
    add x2 -> x0, other arithmetic: 2.34 us -> none  [the longest x1 1.21 us: local(): dual_next = dual_state + scale * residual_dual.reshape(dual_state.shape)]
where the time goes in v2:
time: 60 us; the launch traced here: 59.9 us
  Pallas kernels  59.2 us (99%)
  between operations  0.64 us (1%)
    pallas_call x1, Pallas kernels, local(): pl.pallas_call(functools.partial(kernel, axes), out_shape=(field, field,...  55 us
    pallas_call x1, Pallas kernels, local(): pl.pallas_call(update, grid=(4,), out_shape=(whole, whole), in_specs=[pl....  4.22 us

profile of v2, /device:TPU:0, one launch (start us, length us, event | category | flops | bytes accessed | tf_op | source)
XLA Modules:
  0.0 59.9 jit_solution(8435302300230922033)
XLA Ops:
  0.6 55.0 %shard_map.113 = (f32[137,16,1,128]{3,2,1,0:T(1,128)}, f32[137,16,1,128]{3,2,1,0:T(1,128)}, f32[1,128]{1,0:T(1,128)}) custom-call(f32[137,16,1,128]{3,2,1,0:T(1,128)} %bitcast.16, f32[137,16,1,128]{3,2,1,0:T(1,128)} %bitcast.18, f32[137,16,1,128]{3,2,1,0:T(1,128)} %bitcast.22, f32[137,16,1,128]{3,2,1,0:T(1,128)} %bitcast.23, f32[137,16,1,128]{3,2,1,0:T(1,128)} %bitcast.24, ...), custom_call_target="tpu_custom_call" | custom-call | tf_op jit(solution)/shard_map/pallas_call | solution.py:535
  55.6 4.2 %shard_map.114 = (f32[137,16,128]{2,1,0:T(8,128)}, f32[137,16,128]{2,1,0:T(8,128)}) custom-call(f32[1,1,128]{2,1,0:T(1,128)} %bitcast.29, f32[137,16,128]{2,1,0:T(8,128)} %bitcast.19, f32[137,16,128]{2,1,0:T(8,128)} %bitcast.17, f32[137,16,128]{2,1,0:T(8,128)} %bitcast.20, f32[137,16,128]{2,1,0:T(8,128)} %bitcast.21), custom_call_target="tpu_custom_call" | custom-call | tf_op jit(solution)/shard_map/pallas_call | solution.py:549

commit v3 on v2

--- a/solution.py
+++ b/solution.py
@@ -27,7 +27,7 @@
     q_own, q_left, q_right, outside, q_dual, out_send, x_msg, x_msg_up, x_msg_down,
     pv, pu, pw, pa, pb,
     dual_v, forcing_v, gradient_v, error_v, obs_v, spread, mat_v, spread_v, mat, mat_t, acc, part, parts,
-    load_sem, small_sem, out_sem, u_send, u_recv, e_send, e_recv, o_sem,
+    load_sem, small_sem, u_send, u_recv, e_send, e_recv, o_sem,
     x_send, x_recv, c_send, c_recv, q_send, q_recv, m_send, m_recv, r_send, r_recv, met,
 ):
     windows, nx, ny = axes
@@ -72,11 +72,11 @@
 
     def load(f, i):
         source, home = homes[f]
-        return pltpu.make_async_copy(source.at[:, i, 0], home(i), load_sem.at[f, i])
+        return pltpu.make_async_copy(source.at[:, i, 0], home(i), load_sem.at[f])
 
     def loaded(*which):
         for f in which:
-            loop(rows, lambda i, f=f: load(f, i).wait())
+            pltpu.make_async_copy(homes[f][0], homes[f][0], load_sem.at[f]).wait()
 
     barrier = pltpu.get_barrier_semaphore()
     lines = (("tm", k, windows), ("gx", gx, nx), ("gy", gy, ny))
@@ -126,18 +126,25 @@
         low, high = quads - 1 - q, quads + q
         return (2 * low, 2 * low + 1, 2 * high, 2 * high + 1)
 
-    def dual_copy(i):
-        return remote(dual.at[:, i, 0], inbox.at[i], u_send.at[i], u_recv.at[i], {"tm": k - 1})
-
-    def end_copy(i):
-        return remote(end.at[i], end_in.at[i], e_send.at[i], e_recv.at[i], {"tm": k + 1})
+    def arrived(semaphores, q):
+        whole = dual.at[:, pl.ds(0, 4)]
+        remote(whole, whole, u_send, semaphores.at[q], {"tm": k}).wait_recv()
+
+    def left_all(semaphore):
+        remote(dual, dual, semaphore, u_recv.at[0], {"tm": k}).wait_send()
+
+    def dual_copy(i, q):
+        return remote(dual.at[:, i, 0], inbox.at[i], u_send, u_recv.at[q], {"tm": k - 1})
+
+    def end_copy(i, q):
+        return remote(end.at[i], end_in.at[i], e_send, e_recv.at[q], {"tm": k + 1})
 
     def outside_copy():
         return remote(out_send, outside, o_sem.at[0], o_sem.at[1], {"tm": k - 1})
 
     def send_quad(copy, q):
         for i in quad_rows(q):
-            copy(i).start()
+            copy(i, q).start()
 
     chain = ((v0, v1, v2), (w0, w1, w2))
 
@@ -187,8 +194,11 @@
     def turn(i):
         return GROUP * (i + 2) + RIM
 
-    def pack_into(ref, index, i, value):
-        ref[index] = jnp.where(place == i, pltpu.roll(value, turn(i) % width, 1), ref[index])
+    def pack_into(ref, index, which, value):
+        packed = ref[index]
+        for i in which:
+            packed = jnp.where(place == i, pltpu.roll(value(i), turn(i) % width, 1), packed)
+        ref[index] = packed
 
     inside_x = ((place >= 0) | not_(x_first)) & ((place < rows) | not_(x_last)) & (place < rows + 2)
     own_rows = (place >= 0) & (place < rows)
@@ -287,31 +297,23 @@
 
     def enter(q):
         which = quad_rows(q)
-        for i in which:
-            dual_copy(i).wait_recv()
+        arrived(u_recv, q)
         values = mixed(mat_t, [inbox[i] for i in which])
         for i, value in zip(which, values):
             w0[i + 1] = value
-        for i in which:
-            pack_into(q_dual, 0, i, inbox[i])
-
-    def enter_rim():
-        own, far = q_dual[0], outside[...]
-        assemble(pu, 0, own, far, far)
-
-    def result(ref, out, which, i):
-        return pltpu.make_async_copy(ref.at[i], out.at[:, i, 0], out_sem.at[which, i])
-
-    def square(value):
-        acc[...] += value * value
-
-    def finish_dual(i, earlier):
-        value = forcing_v[i]
+        pack_into(q_dual, 0, which, lambda i: inbox[i])
+
+    def finish(out, which, values):
+        squares = functools.reduce(jnp.add, [value * value for value in values])
+        for i, value in zip(which, values):
+            out[pl.ds(i, levels, stride=rows), :] = value
+        acc[...] += squares
+
+    def finish_dual(q, earlier):
+        which = quad_rows(q)
         if earlier:
-            end_copy(i).wait_recv()
-            value = value + end_in[i]
-            forcing_v[i] = value
-        square(value)
+            arrived(e_recv, q)
+        finish(out_dual, which, [forcing_v[i] + end_in[i] if earlier else forcing_v[i] for i in which])
 
     def early_residuals(i):
         d, v = dual_v[i], v0[i + 1]
@@ -322,7 +324,7 @@
     def _():
         send_quad(dual_copy, quads - 1)
         loaded(3)
-        loop(rows, lambda i: pack_into(q_own, 3, i, dual_v[i]))
+        pack_into(q_own, 3, range(rows), lambda i: dual_v[i])
         start_both(q_up(3), q_down(3), y_first, y_last)
         heard_both(q_up(3), q_down(3), y_first, y_last)
         out_send[...] = jnp.where(near, q_left[3], q_right[3])
@@ -338,7 +340,7 @@
             ((0, lambda i: v0[i + 1]), (1, lambda i: by[i]), (2, lambda i: ax[i + 1]))
         ):
             loaded(f)
-            loop(rows, lambda i, n=n, value=value: pack_into(q_own, n, i, value(i)))
+            pack_into(q_own, n, range(rows), value)
             start_both(q_up(n), q_down(n), y_first, y_last)
 
     pl.when(not_(has_next))(lambda: loaded(0, 1, 2))
@@ -354,23 +356,31 @@
 
         def lower(i):
             back = (2 * width - turn(i)) % width
-            by_low[i] = pltpu.roll(jnp.where(lane == width - 1, pltpu.roll(pb[0, 0], back, 1), by[i]), 1, 1)
-
-        loop(rows, lower)
-        loop(quads - 1, lambda q: forward_quad(0, q))
+            return pltpu.roll(jnp.where(lane == width - 1, pltpu.roll(pb[0, 0], back, 1), by[i]), 1, 1)
+
+        def lower_four(t):
+            four = [4 * t + j for j in range(4)]
+            for i, value in zip(four, [lower(i) for i in four]):
+                by_low[i] = value
+
+        loop(rows // 4, lower_four)
+        for q in range(quads - 1):
+            forward_quad(0, q)
         x_heard(0, 0)
         pl.when(not_(x_first))(lambda: a_up().wait_recv())
         forward_quad(0, quads - 1)
         x_start(0, 1)
         advance_rim(pv, 0, forward_rim, mat)
-        loop(quads - 1, lambda q: forward_quad(1, q))
+        for q in range(quads - 1):
+            forward_quad(1, q)
         advance_rim(pv, 1, forward_rim, mat)
 
         def early_end(q):
             forward_quad(2, q)
             send_quad(end_copy, q)
 
-        loop(quads - 2, early_end)
+        for q in range(quads - 2):
+            early_end(q)
 
         read_message(0, [(ref, 0, side) for ref in (pv, pb, pa) for side in (0, 1)])
         advance_rim(pv, 0, forward_rim, mat)
@@ -389,8 +399,7 @@
 
     @pl.when(not_(has_prev))
     def _():
-        loop(rows, lambda i: finish_dual(i, False))
-        loop(rows, lambda i: result(forcing_v, out_dual, 0, i).start())
+        loop(quads, lambda q: finish_dual(q, False))
 
     pl.semaphore_wait(met.at[0], nx - 1)
     greet(met.at[1], lines[0])
@@ -400,61 +409,62 @@
         enter(quads - 1)
         x_start(1, 0)
         outside_copy().wait_recv()
-        enter_rim()
+        own, far = q_dual[0], outside[...]
+        assemble(pu, 0, own, far, far)
         write_message(1, [pu[0, 0], pu[0, 1]])
         x_heard(0, 2)
         forward_quad(2, quads - 1)
         send_quad(end_copy, quads - 1)
 
-        def rim_start():
-            enter_rim_full()
-            pw[0, 0], pw[0, 1] = mixed(mat_t, [pu[0, 0], pu[0, 1]])
-
-        def enter_rim_full():
+        def enter_rim():
             own, far = q_dual[0], outside[...]
+            both = []
             for side, (left, right) in enumerate(((far, own), (own, far))):
                 value = jnp.where(near, left, right)
                 low = pltpu.roll(x_msg_up[1], (-2 * GROUP * side) % width, 1)
                 high = pltpu.roll(x_msg_down[1], (GROUP * (rows + 2) - 2 * GROUP * side) % width, 1)
                 value = jnp.where(place < 0, low, jnp.where(place >= rows, high, value))
-                pu[0, side] = jnp.where(inside[side], value, 0.0)
-
-        loop(quads - 1, lambda t: enter(quads - 2 - t))
+                both.append(jnp.where(inside[side], value, 0.0))
+            pw[0, 0], pw[0, 1] = mixed(mat_t, both)
+
+        def adjoint_quads(n, which):
+            for q in which:
+                if q == quads - 1:
+                    x_heard(1, n)
+                adjoint_quad(n, q)
+                if q == quads - 1:
+                    x_start(1, n + 1)
+
+        for q in range(quads - 2, 0, -1):
+            enter(q)
         heard_both(m_up(1), m_down(1), x_first, x_last)
-        rim_start()
-        x_heard(1, 0)
-        adjoint_quad(0, quads - 1)
-        x_start(1, 1)
-        loop(quads - 1, lambda t: adjoint_quad(0, t))
+        enter_rim()
+        adjoint_quads(0, range(quads - 1, 1, -1))
         advance_rim(pw, 0, adjoint_rim, mat_t)
-        loop(quads - 1, lambda t: adjoint_quad(1, t))
-        x_heard(1, 1)
-        adjoint_quad(1, quads - 1)
-        x_start(1, 2)
+        adjoint_quads(1, range(quads - 1, 2, -1))
+        enter(0)
+        enter_rim()
+        adjoint_quads(0, range(min(1, quads - 1), -1, -1))
+        advance_rim(pw, 0, adjoint_rim, mat_t)
+        adjoint_quads(1, range(min(2, quads - 1), -1, -1))
         advance_rim(pw, 1, adjoint_rim, mat_t)
-
-        def finish_incr(q):
-            for i in quad_rows(q):
-                value = gradient_v[i] + adjoint_row(w2, (pw[2, 0], pw[2, 1]), i)
-                gradient_v[i] = value
-                square(value)
-
-        loop(quads - 1, finish_incr)
         x_heard(1, 2)
-        finish_incr(quads - 1)
-
-    pl.when(not_(has_next))(lambda: loop(rows, lambda i: square(gradient_v[i])))
-    loop(rows, lambda i: result(gradient_v, out_incr, 1, i).start())
-
-    @pl.when(has_prev)
+        for q in range(quads):
+            which = quad_rows(q)
+            finish(
+                out_incr, which,
+                [gradient_v[i] + adjoint_row(w2, (pw[2, 0], pw[2, 1]), i) for i in which],
+            )
+
+    @pl.when(not_(has_next))
     def _():
         def body(q):
-            for i in quad_rows(q):
-                finish_dual(i, True)
-            for i in quad_rows(q):
-                result(forcing_v, out_dual, 0, i).start()
+            which = quad_rows(q)
+            finish(out_incr, which, [gradient_v[i] for i in which])
 
         loop(quads, body)
+
+    pl.when(has_prev)(lambda: loop(quads, lambda q: finish_dual(q, True)))
 
     pl.semaphore_wait(met.at[1], windows - 1)
     part[...] = jnp.sum(acc[...], axis=0, keepdims=True)
@@ -465,15 +475,11 @@
 
     def tell(d):
         other = (me + d) % count
-        return remote(part, parts.at[me], r_send.at[d], r_recv.at[me], coords(other))
-
-    def hear(d):
-        other = (me + count - d) % count
-        return remote(part, parts.at[other], r_send.at[d], r_recv.at[other], coords(other))
+        return remote(part, parts.at[me], r_send, r_recv, coords(other))
 
     loop(count, lambda d: tell(d).start(), 1)
 
-    pl.when(has_prev)(lambda: loop(rows, lambda i: dual_copy(i).wait_send()))
+    pl.when(has_prev)(lambda: left_all(u_send))
 
     @pl.when(has_prev)
     def _():
@@ -482,7 +488,7 @@
 
     @pl.when(has_next)
     def _():
-        loop(rows, lambda i: end_copy(i).wait_send())
+        left_all(e_send)
         pl.when(not_(x_last))(lambda: a_up().wait_send())
         for n in range(STEPS):
             sent_both(x_up(0, n), x_down(0, n), x_first, x_last)
@@ -491,19 +497,30 @@
         for n in range(2):
             sent_both(m_up(n), m_down(n), x_first, x_last)
 
-    for ref, out, which in ((forcing_v, out_dual, 0), (gradient_v, out_incr, 1)):
-        loop(rows, lambda i: result(ref, out, which, i).wait())
-    loop(count, lambda d: hear(d).wait_recv(), 1)
+    others = parts.at[pl.ds(0, count - 1)]
+    every = remote(others, others, r_send, r_recv, {"tm": k})
+    every.wait_recv()
     total = jnp.sum(jnp.sum(parts[...], axis=0), axis=1, keepdims=True)
     cells = 2 * rows * levels * width * count
     root_mean = jnp.sqrt(total / cells + 1e-06)
     out_scale[...] = jnp.broadcast_to(jnp.minimum(1.0, 0.5 / root_mean), out_scale.shape)
-    loop(count, lambda d: tell(d).wait_send(), 1)
-
-
-def update(scale, dual, increment, residual_dual, residual_incr, dual_next, increment_next):
-    dual_next[...] = dual[...] + scale[...] * residual_dual[...]
-    increment_next[...] = increment[...] + scale[...] * residual_incr[...]
+    every.wait_send()
+
+
+def update(scale, dual, increment, residual_dual, residual_incr, dual_next, incr_next, dual_v, incr_v, sem):
+    size = dual.shape[0]
+    chunk = -(-size // (4 * 8)) * 8
+    copies = []
+    for lot, start in enumerate(range(0, size, chunk)):
+        span = pl.ds(start, min(chunk, size - start))
+        for j, (now, rest, home, out) in enumerate((
+            (dual, residual_dual, dual_v, dual_next), (increment, residual_incr, incr_v, incr_next)
+        )):
+            home[span, :] = now[span, :] + scale[...] * rest[span, :]
+            copies.append(pltpu.make_async_copy(home.at[span], out.at[span], sem.at[j, lot]))
+            copies[-1].start()
+    for copy in copies:
+        copy.wait()
 
 
 def local(axes, increment, dual_state, forcing, gradient, courant_x, courant_y, error_var, obs_weight, diffusion, level_mix):
@@ -515,6 +532,7 @@
         part.reshape(levels, rows, 1, width)
         for part in (increment, dual_state, forcing, gradient, courant_x, courant_y, error_var, obs_weight)
     ]
+    fields = [pltpu.with_memory_space_constraint(part, pltpu.HBM) for part in fields]
     slab = lambda *lead: pltpu.VMEM((*lead, levels, width), jnp.float32)
     dma = lambda *shape: pltpu.SemaphoreType.DMA(shape)
     one = pltpu.SemaphoreType.DMA
@@ -526,33 +544,32 @@
         slab(), pltpu.VMEM((levels, levels), jnp.float32), pltpu.VMEM((1, levels), jnp.float32),
         pltpu.VMEM((2 * stack, levels), jnp.bfloat16), pltpu.VMEM((2 * stack, levels), jnp.bfloat16),
         slab(), pltpu.VMEM((1, width), jnp.float32), pltpu.VMEM((count, 1, width), jnp.float32),
-        dma(FIELDS, rows), dma(2), dma(2, rows), dma(rows), dma(rows), dma(rows), dma(rows), dma(2),
+        dma(FIELDS), dma(2), one, dma(rows // 4), one, dma(rows // 4), dma(2),
         dma(2, STEPS, 2), dma(2, STEPS, 2), one, one, dma(4, 2), dma(4, 2), dma(2, 2), dma(2, 2),
-        dma(count), dma(count), pltpu.SemaphoreType.REGULAR((2,)),
+        one, one, pltpu.SemaphoreType.REGULAR((2,)),
     ]
-    field = jax.ShapeDtypeStruct((levels, rows, 1, width), jnp.float32)
+    field = jax.ShapeDtypeStruct((levels * rows, width), jnp.float32)
+    vmem = pl.BlockSpec(memory_space=pltpu.VMEM)
     anywhere = pl.BlockSpec(memory_space=pltpu.HBM)
     residual_dual, residual_incr, scale = pl.pallas_call(
         functools.partial(kernel, axes),
         out_shape=(field, field, jax.ShapeDtypeStruct((1, width), jnp.float32)),
         in_specs=[anywhere] * 10,
-        out_specs=(anywhere, anywhere, pl.BlockSpec(memory_space=pltpu.VMEM)),
+        out_specs=(vmem, vmem, vmem),
         scratch_shapes=scratch,
         compiler_params=pltpu.CompilerParams(
-            collective_id=0, has_side_effects=True, vmem_limit_bytes=63 * 1024 * 1024
+            collective_id=0, has_side_effects=True, vmem_limit_bytes=32 * 1024 * 1024
         ),
-    )(*fields, diffusion[None, :], level_mix)
-    flat = lambda part: part.reshape(levels, rows, width)
-    chunk = -(-levels // 4)
-    block = pl.BlockSpec((chunk, rows, width), lambda i: (i, 0, 0))
-    whole = jax.ShapeDtypeStruct((levels, rows, width), jnp.float32)
+    )(*fields, *(pltpu.with_memory_space_constraint(part, pltpu.HBM) for part in (diffusion[None, :], level_mix)))
+    flat = lambda part: part.reshape(levels * rows, width)
     results = pl.pallas_call(
         update,
-        grid=(4,),
-        out_shape=(whole, whole),
-        in_specs=[pl.BlockSpec((1, 1, width), lambda i: (0, 0, 0))] + [block] * 4,
-        out_specs=(block, block),
-    )(scale.reshape(1, 1, width), *map(flat, (dual_state, increment, residual_dual, residual_incr)))
+        out_shape=(field, field),
+        in_specs=[vmem] * 5,
+        out_specs=(anywhere, anywhere),
+        scratch_shapes=[pltpu.VMEM(field.shape, jnp.float32)] * 2 + [dma(2, 4)],
+        compiler_params=pltpu.CompilerParams(vmem_limit_bytes=16 * 1024 * 1024),
+    )(scale, flat(dual_state), flat(increment), residual_dual, residual_incr)
     return tuple(part.reshape(increment.shape) for part in results)
 
 

time: 60 us -> 49.1 us (0.82)
  Pallas kernels: 59.2 us -> 48.2 us
    pallas_call x1, Pallas kernels: 55 us -> 46.7 us  [local(): pl.pallas_call(functools.partial(kernel, axes), out_shape=(field, field,...]
    pallas_call x1, Pallas kernels: 4.22 us -> 1.47 us  [local(): pl.pallas_call(update, out_shape=(field, field), in_specs=[vmem] * 5, out...]
where the time goes in v3:
time: 49.1 us; the launch traced here: 49 us
  Pallas kernels  48.2 us (98%)
  between operations  0.83 us (2%)
    pallas_call x1, Pallas kernels, local(): pl.pallas_call(functools.partial(kernel, axes), out_shape=(field, field,...  46.7 us
    pallas_call x1, Pallas kernels, local(): pl.pallas_call(update, out_shape=(field, field), in_specs=[vmem] * 5, out...  1.47 us

profile of v3, /device:TPU:0, one launch (start us, length us, event | category | flops | bytes accessed | tf_op | source)
XLA Modules:
  0.0 49.0 jit_solution(14550621083914063293)
XLA Ops:
  0.6 0.0 copy-start
  0.6 0.0 copy-start.1
  0.7 46.7 %shard_map.113 = (f32[2192,128]{1,0:T(8,128)S(1)}, f32[2192,128]{1,0:T(8,128)S(1)}, f32[1,128]{1,0:T(1,128)S(1)}) custom-call(f32[137,16,1,128]{3,2,1,0:T(1,128)} %bitcast.13, f32[137,16,1,128]{3,2,1,0:T(1,128)} %bitcast.15, f32[137,16,1,128]{3,2,1,0:T(1,128)} %bitcast.17, f32[137,16,1,128]{3,2,1,0:T(1,128)} %bitcast.18, f32[137,16,1,128]{3,2,1,0:T(1,128)} %bitcast.19, ...), custom_call_target="tpu_custom_call" | custom-call | tf_op jit(solution)/shard_map/pallas_call | solution.py:554
  47.3 0.0 copy-done
  47.4 0.0 copy-done.1
  47.4 1.5 %shard_map.114 = (f32[2192,128]{1,0:T(8,128)}, f32[2192,128]{1,0:T(8,128)}) custom-call(f32[1,128]{1,0:T(1,128)S(1)} %get-tuple-element.7.scale, f32[2192,128]{1,0:T(8,128)S(1)} %bitcast.16, f32[2192,128]{1,0:T(8,128)S(1)} %bitcast.14, f32[2192,128]{1,0:T(8,128)S(1)} %get-tuple-element.8.residual_dual, f32[2192,128]{1,0:T(8,128)S(1)} %get-tuple-element.9.residual_incr), custom_call_target="tpu_custom_call" | custom-call | tf_op jit(solution)/shard_map/pallas_call | solution.py:565
Async XLA Ops:
  0.6 46.7 %copy-start = (f32[1,137,16,128]{3,2,1,0:T(8,128)S(1)}, f32[1,137,16,128]{3,2,1,0:T(8,128)}, u32[]{:S(2)}) copy-start(f32[1,137,16,128]{3,2,1,0:T(8,128)} %param.10) | copy-start | bytes 3366916
  0.6 46.7 %copy-start.1 = (f32[1,137,16,128]{3,2,1,0:T(8,128)S(1)}, f32[1,137,16,128]{3,2,1,0:T(8,128)}, u32[]{:S(2)}) copy-start(f32[1,137,16,128]{3,2,1,0:T(8,128)} %param.11) | copy-start | bytes 3366916

commit v4 on v3

--- a/solution.py
+++ b/solution.py
@@ -23,18 +23,18 @@
     axes,
     increment, dual, forcing, gradient, courant_x, courant_y, error_var, obs_weight, spread_row, matrix,
     out_dual, out_incr, out_scale,
-    v0, v1, v2, w0, w1, w2, ax, by, by_low, inbox, end, end_in,
+    v0, v1, v2, w0, w1, w2, ax, by, inbox, end, end_in,
     q_own, q_left, q_right, outside, q_dual, out_send, x_msg, x_msg_up, x_msg_down,
     pv, pu, pw, pa, pb,
-    dual_v, forcing_v, gradient_v, error_v, obs_v, spread, mat_v, spread_v, mat, mat_t, acc, part, parts,
+    dual_v, forcing_v, gradient_v, error_v, obs_v, spread, mat_v, spread_v, mat, mat_t, x_high, x_low, acc, part, parts,
     load_sem, small_sem, u_send, u_recv, e_send, e_recv, o_sem,
     x_send, x_recv, c_send, c_recv, q_send, q_recv, m_send, m_recv, r_send, r_recv, met,
 ):
     windows, nx, ny = axes
     count = windows * nx * ny
     rows, levels, width = dual_v.shape
-    pairs = rows // 2
-    quads = pairs // 2
+    reach = rows // 2
+    spans = [slice(low, min(low + 16, levels)) for low in range(0, levels, 16)]
     stack = mat.shape[0] // 2
     k, gx, gy = lax.axis_index("tm"), lax.axis_index("gx"), lax.axis_index("gy")
     me = (k * nx + gx) * ny + gy
@@ -122,13 +122,19 @@
 
     pl.semaphore_wait(barrier, windows + nx + ny - 3)
 
-    def quad_rows(q):
-        low, high = quads - 1 - q, quads + q
-        return (2 * low, 2 * low + 1, 2 * high, 2 * high + 1)
-
-    def arrived(semaphores, q):
-        whole = dual.at[:, pl.ds(0, 4)]
-        remote(whole, whole, u_send, semaphores.at[q], {"tm": k}).wait_recv()
+    def mirror(*steps):
+        return [i for j in steps for i in (reach - 1 - j, reach + j)]
+
+    def paired(steps):
+        steps = list(steps)
+        return [steps[t : t + 2] for t in range(0, len(steps), 2)]
+
+    outward = [[0]] + paired(range(1, reach))
+    inward = paired(range(reach - 1, 1, -1)) + [[1], [0]]
+
+    def arrived(semaphores, lot, size):
+        whole = dual.at[:, pl.ds(0, size)]
+        remote(whole, whole, u_send, semaphores.at[lot], {"tm": k}).wait_recv()
 
     def left_all(semaphore):
         remote(dual, dual, semaphore, u_recv.at[0], {"tm": k}).wait_send()
@@ -142,9 +148,10 @@
     def outside_copy():
         return remote(out_send, outside, o_sem.at[0], o_sem.at[1], {"tm": k - 1})
 
-    def send_quad(copy, q):
-        for i in quad_rows(q):
-            copy(i, q).start()
+    def send_duals(lots):
+        for lot in lots:
+            for i in mirror(*inward[lot]):
+                dual_copy(i, lot).start()
 
     chain = ((v0, v1, v2), (w0, w1, w2))
 
@@ -195,10 +202,11 @@
         return GROUP * (i + 2) + RIM
 
     def pack_into(ref, index, which, value):
-        packed = ref[index]
-        for i in which:
-            packed = jnp.where(place == i, pltpu.roll(value(i), turn(i) % width, 1), packed)
-        ref[index] = packed
+        for lv in spans:
+            packed = ref[index, lv]
+            for i in which:
+                packed = jnp.where(place[lv] == i, pltpu.roll(value(i, lv), turn(i) % width, 1), packed)
+            ref[index, lv] = packed
 
     inside_x = ((place >= 0) | not_(x_first)) & ((place < rows) | not_(x_last)) & (place < rows + 2)
     own_rows = (place >= 0) & (place < rows)
@@ -229,33 +237,56 @@
             value = jnp.where(place < 0, low, jnp.where(place >= rows, high, ref[index, side]))
             ref[index, side] = jnp.where(inside[side], value, 0.0)
 
-    def mixed(mats, blocks):
-        high, low = split(jnp.concatenate(blocks, axis=1))
+    turns = [0]
+
+    def mixed(mats, rule, size, put):
+        turns[0] = 1 - turns[0]
+        highs, lows = x_high.at[turns[0]], x_low.at[turns[0]]
+        for lv in spans:
+            for j, value in enumerate(rule(lv)):
+                highs[lv, j * width : (j + 1) * width], lows[lv, j * width : (j + 1) * width] = split(value)
         dot = functools.partial(jnp.dot, preferred_element_type=jnp.float32)
-        wide = dot(mats[...], high)
-        result = dot(mats[0:levels, :], low) + wide[stack : stack + levels] + wide[0:levels]
-        return [result[:, j * width : (j + 1) * width] for j in range(len(blocks))]
-
-    def sides(block, left_rim, right_rim, i):
-        back = (2 * width - turn(i)) % width
-        left = pltpu.roll(jnp.where(lane == width - 1, pltpu.roll(left_rim, back, 1), block), 1, 1)
-        right = pltpu.roll(jnp.where(lane == 0, pltpu.roll(right_rim, back, 1), block), width - 1, 1)
-        return left, right
-
-    def forward_row(state, rim, i):
-        v, before, after = state[i + 1], state[i], state[i + 2]
-        left, right = sides(v, rim[0], rim[1], i)
-        s = spread[...]
-        flow = (1.0 - 4.0 * s - ax[i + 1] - by[i]) * v + ax[i] * before + by_low[i] * left
-        return flow + s * (before + after + left + right)
-
-    def adjoint_row(state, rim, i):
-        w, before, after = state[i + 1], state[i], state[i + 2]
-        left, right = sides(w, rim[0], rim[1], i)
-        s = spread[...]
-        a, b = ax[i + 1], by[i]
-        flow = (1.0 - 4.0 * s - a - b) * w + a * after + b * right
-        return flow + s * (before + after + left + right)
+        top, rest = mats.at[0:levels], mats.at[stack : stack + levels]
+        for j in range(0, size, 2):
+            here = slice(j * width, (j + 2) * width)
+            result = dot(top[...], lows[:, here]) + dot(rest[...], highs[:, here]) + dot(top[...], highs[:, here])
+            put(j, result[:, :width])
+            put(j + 1, result[:, width:])
+
+    def back(i):
+        return (2 * width - turn(i)) % width
+
+    def from_left(block, rim, i, lv):
+        return pltpu.roll(jnp.where(lane[lv] == width - 1, pltpu.roll(rim, back(i), 1), block), 1, 1)
+
+    def from_right(block, rim, i, lv):
+        return pltpu.roll(jnp.where(lane[lv] == 0, pltpu.roll(rim, back(i), 1), block), width - 1, 1)
+
+    def forward_rows(n, which, lv):
+        state, s = chain[0][n], spread[lv]
+        keep = 1.0 - 4.0 * s
+        values = []
+        for i in which:
+            v, before, after = state[i + 1, lv], state[i, lv], state[i + 2, lv]
+            b = by[i, lv]
+            left = from_left((b + s) * v, (pb[0, 0, lv] + s) * pv[n, 0, lv], i, lv)
+            right = from_right(v, pv[n, 1, lv], i, lv)
+            flow = (keep - ax[i + 1, lv] - b) * v + ax[i, lv] * before + left
+            values.append(flow + s * (before + after + right))
+        return values
+
+    def adjoint_rows(n, which, lv):
+        state, s = chain[1][n], spread[lv]
+        keep = 1.0 - 4.0 * s
+        values = []
+        for i in which:
+            w, before, after = state[i + 1, lv], state[i, lv], state[i + 2, lv]
+            left = from_left(w, pw[n, 0, lv], i, lv)
+            right = from_right(w, pw[n, 1, lv], i, lv)
+            a, b = ax[i + 1, lv], by[i, lv]
+            flow = (keep - a - b) * w + a * after + b * right
+            values.append(flow + s * (before + after + left + right))
+        return values
 
     def rim_parts(block):
         return (
@@ -263,57 +294,132 @@
             pltpu.roll(block, 1, 1), pltpu.roll(block, width - 1, 1),
         )
 
-    def forward_rim(block, side):
+    def forward_rim(block, side, lv):
         before, after, left, right = rim_parts(block)
-        s, a, b = spread[...], pa[0, side], pb[0, side]
+        s, a, b = spread[lv], pa[0, side, lv], pb[0, side, lv]
         flow = (1.0 - 4.0 * s - a - b) * block
         flow = flow + pltpu.roll(a, GROUP, 1) * before + pltpu.roll(b, 1, 1) * left
-        return jnp.where(inside[side], flow + s * (before + after + left + right), 0.0)
-
-    def adjoint_rim(block, side):
+        return jnp.where(inside[side][lv], flow + s * (before + after + left + right), 0.0)
+
+    def adjoint_rim(block, side, lv):
         before, after, left, right = rim_parts(block)
-        s, a, b = spread[...], pa[0, side], pb[0, side]
+        s, a, b = spread[lv], pa[0, side, lv], pb[0, side, lv]
         flow = (1.0 - 4.0 * s - a - b) * block + a * after + b * right
-        return jnp.where(inside[side], flow + s * (before + after + left + right), 0.0)
+        return jnp.where(inside[side][lv], flow + s * (before + after + left + right), 0.0)
+
+    def put_all(state, shift, which, rims=None, n=0):
+        def put(j, value):
+            if j < len(which):
+                state[which[j] + shift] = value
+            else:
+                rims[n, j - len(which)] = value
+
+        return put
 
     def advance_rim(ref, n, rule, mats):
-        both = mixed(mats, [rule(ref[n, 0], 0), rule(ref[n, 1], 1)])
-        ref[n + 1, 0], ref[n + 1, 1] = both
-
-    def forward_quad(n, q):
-        which = quad_rows(q)
-        values = mixed(mat, [forward_row(chain[0][n], (pv[n, 0], pv[n, 1]), i) for i in which])
-        for i, value in zip(which, values):
-            if n == STEPS - 1:
-                end[i] = value
-            else:
-                chain[0][n + 1][i + 1] = value
-
-    def adjoint_quad(n, q):
-        which = quad_rows(q)
-        values = mixed(mat_t, [adjoint_row(chain[1][n], (pw[n, 0], pw[n, 1]), i) for i in which])
-        for i, value in zip(which, values):
-            chain[1][n + 1][i + 1] = value
-
-    def enter(q):
-        which = quad_rows(q)
-        arrived(u_recv, q)
-        values = mixed(mat_t, [inbox[i] for i in which])
-        for i, value in zip(which, values):
-            w0[i + 1] = value
-        pack_into(q_dual, 0, which, lambda i: inbox[i])
+        mixed(mats, lambda lv: [rule(ref[n, side, lv], side, lv) for side in (0, 1)], 2, put_all(None, 0, [], ref, n + 1))
+
+    def forward(n, steps, rim):
+        which = mirror(*steps)
+        target = (end, 0) if n == STEPS - 1 else (chain[0][n + 1], 1)
+
+        def rule(lv):
+            return forward_rows(n, which, lv) + [forward_rim(pv[n, side, lv], side, lv) for side in (0, 1) if rim]
+
+        mixed(mat, rule, len(which) + 2 * rim, put_all(*target, which, pv, n + 1))
+
+    def adjoint(n, steps, rim):
+        which = mirror(*steps)
+        if n == STEPS - 1:
+            def body(t):
+                pair = mirror(steps[0] - t)
+                finish(out_incr, pair, lambda lv: [
+                    gradient_v[i, lv] + value for i, value in zip(pair, adjoint_rows(n, pair, lv))
+                ])
+
+            loop(len(steps), body)
+        else:
+            def rule(lv):
+                return adjoint_rows(n, which, lv) + [adjoint_rim(pw[n, side, lv], side, lv) for side in (0, 1) if rim]
+
+            mixed(mat_t, rule, len(which) + 2 * rim, put_all(chain[1][n + 1], 1, which, pw, n + 1))
+
+    def rim_entry(lv):
+        own, far = q_dual[0, lv], outside[lv]
+        both = []
+        for side, (left, right) in enumerate(((far, own), (own, far))):
+            value = jnp.where(near[lv], left, right)
+            low = pltpu.roll(x_msg_up[1, lv], (-2 * GROUP * side) % width, 1)
+            high = pltpu.roll(x_msg_down[1, lv], (GROUP * (rows + 2) - 2 * GROUP * side) % width, 1)
+            value = jnp.where(place[lv] < 0, low, jnp.where(place[lv] >= rows, high, value))
+            both.append(jnp.where(inside[side][lv], value, 0.0))
+        return both
+
+    def enter(lot):
+        which = mirror(*inward[lot])
+        arrived(u_recv, lot, len(which))
+        pack_into(q_dual, 0, which, lambda i, lv: inbox[i, lv])
+        if lot == 1:
+            heard_both(m_up(1), m_down(1), x_first, x_last)
+        rim = lot > 0
+
+        def rule(lv):
+            return [inbox[i, lv] for i in which] + (rim_entry(lv) if rim else [])
+
+        mixed(mat_t, rule, len(which) + 2 * rim, put_all(w0, 1, which, pw, 0))
+
+    done = [0] * STEPS
+
+    def produce(n, steps):
+        if n:
+            while done[n - 1] < min(steps[-1] + 2, reach):
+                first = done[n - 1]
+                produce(n - 1, range(first, min(first + 2, reach)))
+        edge = steps[-1] == reach - 1
+        if edge:
+            if n == 0:
+                write_message(0, [ref[0, side] for ref in (pv, pb, pa) for side in (0, 1)])
+                pl.when(not_(x_first))(lambda: a_up().wait_recv())
+            if n == 1:
+                read_message(0, [(ref, 0, side) for ref in (pv, pb, pa) for side in (0, 1)])
+            x_heard(0, n)
+        if n == 1 and edge:
+            advance_rim(pv, 0, forward_rim, mat)
+        first = done[n]
+        done[n] += len(steps)
+        rim = (n == 0 and first < 3 <= done[n]) or (n == 1 and (first == 0 or edge))
+        forward(n, steps, False)
+        if rim:
+            advance_rim(pv, n, forward_rim, mat)
+        if edge and n < STEPS - 1:
+            x_start(0, n + 1)
+
+    def produce_end(lot):
+        produce(STEPS - 1, outward[lot])
+        for i in mirror(*outward[lot]):
+            end_copy(i, lot).start()
 
     def finish(out, which, values):
-        squares = functools.reduce(jnp.add, [value * value for value in values])
-        for i, value in zip(which, values):
-            out[pl.ds(i, levels, stride=rows), :] = value
-        acc[...] += squares
-
-    def finish_dual(q, earlier):
-        which = quad_rows(q)
+        sums = {}
+        for lv in spans:
+            size = lv.stop - lv.start
+            for i, value in zip(which, values(lv)):
+                out[pl.ds(lv.start * rows + i, size, stride=rows), :] = value
+                sums[size] = sums[size] + value * value if size in sums else value * value
+        for size, value in sums.items():
+            acc[0:size] += value
+
+    def finish_dual(lot, earlier):
         if earlier:
-            arrived(e_recv, q)
-        finish(out_dual, which, [forcing_v[i] + end_in[i] if earlier else forcing_v[i] for i in which])
+            arrived(e_recv, lot, 2 * len(outward[lot]))
+
+        def body(t):
+            pair = mirror(outward[lot][0] + t)
+            finish(out_dual, pair, lambda lv: [
+                forcing_v[i, lv] + end_in[i, lv] if earlier else forcing_v[i, lv] for i in pair
+            ])
+
+        loop(len(outward[lot]), body)
 
     def early_residuals(i):
         d, v = dual_v[i], v0[i + 1]
@@ -322,22 +428,21 @@
 
     @pl.when(has_prev)
     def _():
-        send_quad(dual_copy, quads - 1)
+        send_duals([0])
         loaded(3)
-        pack_into(q_own, 3, range(rows), lambda i: dual_v[i])
+        pack_into(q_own, 3, range(rows), lambda i, lv: dual_v[i, lv])
         start_both(q_up(3), q_down(3), y_first, y_last)
         heard_both(q_up(3), q_down(3), y_first, y_last)
         out_send[...] = jnp.where(near, q_left[3], q_right[3])
-        send_quad(dual_copy, quads - 2)
         outside_copy().start()
-        loop(quads - 2, lambda t: send_quad(dual_copy, quads - 3 - t))
+        send_duals(range(1, len(inward)))
 
     @pl.when(has_next)
     def _():
         x_start(0, 0)
         pl.when(not_(x_last))(lambda: a_up().start())
         for n, (f, value) in enumerate(
-            ((0, lambda i: v0[i + 1]), (1, lambda i: by[i]), (2, lambda i: ax[i + 1]))
+            ((0, lambda i, lv: v0[i + 1, lv]), (1, lambda i, lv: by[i, lv]), (2, lambda i, lv: ax[i + 1, lv]))
         ):
             loaded(f)
             pack_into(q_own, n, range(rows), value)
@@ -352,43 +457,8 @@
         for n, ref in enumerate((pv, pb, pa)):
             heard_both(q_up(n), q_down(n), y_first, y_last)
             assemble(ref, 0, q_own[n], q_left[n], q_right[n])
-        write_message(0, [ref[0, side] for ref in (pv, pb, pa) for side in (0, 1)])
-
-        def lower(i):
-            back = (2 * width - turn(i)) % width
-            return pltpu.roll(jnp.where(lane == width - 1, pltpu.roll(pb[0, 0], back, 1), by[i]), 1, 1)
-
-        def lower_four(t):
-            four = [4 * t + j for j in range(4)]
-            for i, value in zip(four, [lower(i) for i in four]):
-                by_low[i] = value
-
-        loop(rows // 4, lower_four)
-        for q in range(quads - 1):
-            forward_quad(0, q)
-        x_heard(0, 0)
-        pl.when(not_(x_first))(lambda: a_up().wait_recv())
-        forward_quad(0, quads - 1)
-        x_start(0, 1)
-        advance_rim(pv, 0, forward_rim, mat)
-        for q in range(quads - 1):
-            forward_quad(1, q)
-        advance_rim(pv, 1, forward_rim, mat)
-
-        def early_end(q):
-            forward_quad(2, q)
-            send_quad(end_copy, q)
-
-        for q in range(quads - 2):
-            early_end(q)
-
-        read_message(0, [(ref, 0, side) for ref in (pv, pb, pa) for side in (0, 1)])
-        advance_rim(pv, 0, forward_rim, mat)
-        x_heard(0, 1)
-        forward_quad(1, quads - 1)
-        x_start(0, 2)
-        advance_rim(pv, 1, forward_rim, mat)
-        early_end(quads - 2)
+        for lot in range(len(outward) - 2):
+            produce_end(lot)
 
     for f in range(3, FIELDS):
         if f == 3:
@@ -399,72 +469,52 @@
 
     @pl.when(not_(has_prev))
     def _():
-        loop(quads, lambda q: finish_dual(q, False))
+        for lot in range(len(outward)):
+            finish_dual(lot, False)
 
     pl.semaphore_wait(met.at[0], nx - 1)
     greet(met.at[1], lines[0])
 
     @pl.when(has_next)
     def _():
-        enter(quads - 1)
+        enter(0)
         x_start(1, 0)
+        produce_end(len(outward) - 2)
         outside_copy().wait_recv()
         own, far = q_dual[0], outside[...]
         assemble(pu, 0, own, far, far)
         write_message(1, [pu[0, 0], pu[0, 1]])
-        x_heard(0, 2)
-        forward_quad(2, quads - 1)
-        send_quad(end_copy, quads - 1)
-
-        def enter_rim():
-            own, far = q_dual[0], outside[...]
-            both = []
-            for side, (left, right) in enumerate(((far, own), (own, far))):
-                value = jnp.where(near, left, right)
-                low = pltpu.roll(x_msg_up[1], (-2 * GROUP * side) % width, 1)
-                high = pltpu.roll(x_msg_down[1], (GROUP * (rows + 2) - 2 * GROUP * side) % width, 1)
-                value = jnp.where(place < 0, low, jnp.where(place >= rows, high, value))
-                both.append(jnp.where(inside[side], value, 0.0))
-            pw[0, 0], pw[0, 1] = mixed(mat_t, both)
-
-        def adjoint_quads(n, which):
-            for q in which:
-                if q == quads - 1:
-                    x_heard(1, n)
-                adjoint_quad(n, q)
-                if q == quads - 1:
-                    x_start(1, n + 1)
-
-        for q in range(quads - 2, 0, -1):
-            enter(q)
-        heard_both(m_up(1), m_down(1), x_first, x_last)
-        enter_rim()
-        adjoint_quads(0, range(quads - 1, 1, -1))
-        advance_rim(pw, 0, adjoint_rim, mat_t)
-        adjoint_quads(1, range(quads - 1, 2, -1))
-        enter(0)
-        enter_rim()
-        adjoint_quads(0, range(min(1, quads - 1), -1, -1))
-        advance_rim(pw, 0, adjoint_rim, mat_t)
-        adjoint_quads(1, range(min(2, quads - 1), -1, -1))
-        advance_rim(pw, 1, adjoint_rim, mat_t)
-        x_heard(1, 2)
-        for q in range(quads):
-            which = quad_rows(q)
-            finish(
-                out_incr, which,
-                [gradient_v[i] + adjoint_row(w2, (pw[2, 0], pw[2, 1]), i) for i in which],
-            )
+        floor = [reach] * STEPS
+        for lot in range(1, len(inward)):
+            enter(lot)
+            least = inward[lot][-1]
+            for n in range(min(lot, STEPS) if least else STEPS):
+                low = least + 1 + n if least else 0
+                lots = paired(range(floor[n] - 1, low - 1, -1))
+                for t, steps in enumerate(lots):
+                    edge = steps[0] == reach - 1
+                    if edge:
+                        x_heard(1, n)
+                    adjoint(n, steps, t == len(lots) - 1)
+                    if edge and n < STEPS - 1:
+                        x_start(1, n + 1)
+                floor[n] = min(floor[n], low)
+            if lot == 1:
+                produce_end(len(outward) - 1)
 
     @pl.when(not_(has_next))
     def _():
-        def body(q):
-            which = quad_rows(q)
-            finish(out_incr, which, [gradient_v[i] for i in which])
-
-        loop(quads, body)
-
-    pl.when(has_prev)(lambda: loop(quads, lambda q: finish_dual(q, True)))
+        for lot in range(len(outward)):
+            def body(t):
+                pair = mirror(outward[lot][0] + t)
+                finish(out_incr, pair, lambda lv: [gradient_v[i, lv] for i in pair])
+
+            loop(len(outward[lot]), body)
+
+    @pl.when(has_prev)
+    def _():
+        for lot in range(len(outward)):
+            finish_dual(lot, True)
 
     pl.semaphore_wait(met.at[1], windows - 1)
     part[...] = jnp.sum(acc[...], axis=0, keepdims=True)
@@ -516,7 +566,9 @@
         for j, (now, rest, home, out) in enumerate((
             (dual, residual_dual, dual_v, dual_next), (increment, residual_incr, incr_v, incr_next)
         )):
-            home[span, :] = now[span, :] + scale[...] * rest[span, :]
+            for low in range(start, min(start + chunk, size), 64):
+                piece = pl.ds(low, min(64, start + chunk - low, size - low))
+                home[piece, :] = now[piece, :] + scale[...] * rest[piece, :]
             copies.append(pltpu.make_async_copy(home.at[span], out.at[span], sem.at[j, lot]))
             copies[-1].start()
     for copy in copies:
@@ -527,7 +579,8 @@
     levels, rows, width = increment.shape[1:]
     count = axes[0] * axes[1] * axes[2]
     stack = -(-levels // 16) * 16
-    assert rows % 4 == 0 and GROUP * (rows + 4) <= width
+    reach = rows // 2
+    assert rows % 4 == 0 and rows >= 8 and GROUP * (rows + 4) <= width
     fields = [
         part.reshape(levels, rows, 1, width)
         for part in (increment, dual_state, forcing, gradient, courant_x, courant_y, error_var, obs_weight)
@@ -537,14 +590,15 @@
     dma = lambda *shape: pltpu.SemaphoreType.DMA(shape)
     one = pltpu.SemaphoreType.DMA
     scratch = [
-        *[slab(rows + 2)] * 6, slab(rows + 1), slab(rows), slab(rows), slab(rows), slab(rows), slab(rows),
+        *[slab(rows + 2)] * 6, slab(rows + 1), slab(rows), slab(rows), slab(rows), slab(rows),
         slab(4), slab(4), slab(4), slab(), slab(1), slab(), slab(2, 2), slab(2), slab(2),
         slab(3, 2), slab(1, 2), slab(3, 2), slab(1, 2), slab(1, 2),
         slab(rows), slab(rows), slab(rows), slab(rows), slab(rows),
         slab(), pltpu.VMEM((levels, levels), jnp.float32), pltpu.VMEM((1, levels), jnp.float32),
         pltpu.VMEM((2 * stack, levels), jnp.bfloat16), pltpu.VMEM((2 * stack, levels), jnp.bfloat16),
-        slab(), pltpu.VMEM((1, width), jnp.float32), pltpu.VMEM((count, 1, width), jnp.float32),
-        dma(FIELDS), dma(2), one, dma(rows // 4), one, dma(rows // 4), dma(2),
+        *[pltpu.VMEM((2, levels, 8 * width), jnp.bfloat16)] * 2,
+        pltpu.VMEM((16, width), jnp.float32), pltpu.VMEM((1, width), jnp.float32), pltpu.VMEM((count, 1, width), jnp.float32),
+        dma(FIELDS), dma(2), one, dma(reach), one, dma(reach), dma(2),
         dma(2, STEPS, 2), dma(2, STEPS, 2), one, one, dma(4, 2), dma(4, 2), dma(2, 2), dma(2, 2),
         one, one, pltpu.SemaphoreType.REGULAR((2,)),
     ]

time: 49.1 us -> 67.6 us (1.38)
  Pallas kernels: 48.2 us -> 66.6 us
    pallas_call x1, Pallas kernels: 46.7 us -> 65.1 us  [local(): pl.pallas_call(functools.partial(kernel, axes), out_shape=(field, field,...]
where the time goes in v4:
time: 67.6 us; the launch traced here: 67.4 us
  Pallas kernels  66.6 us (99%)
  between operations  0.83 us (1%)
    pallas_call x1, Pallas kernels, local(): pl.pallas_call(functools.partial(kernel, axes), out_shape=(field, field,...  65.1 us
    pallas_call x1, Pallas kernels, local(): pl.pallas_call(update, out_shape=(field, field), in_specs=[vmem] * 5, out...  1.47 us

profile of v4, /device:TPU:0, one launch (start us, length us, event | category | flops | bytes accessed | tf_op | source)
XLA Modules:
  0.0 67.4 jit_solution(2236170463723830304)
XLA Ops:
  0.6 0.0 copy-start
  0.6 0.0 copy-start.1
  0.7 65.1 %shard_map.113 = (f32[2192,128]{1,0:T(8,128)S(1)}, f32[2192,128]{1,0:T(8,128)S(1)}, f32[1,128]{1,0:T(1,128)S(1)}) custom-call(f32[137,16,1,128]{3,2,1,0:T(1,128)} %bitcast.13, f32[137,16,1,128]{3,2,1,0:T(1,128)} %bitcast.15, f32[137,16,1,128]{3,2,1,0:T(1,128)} %bitcast.17, f32[137,16,1,128]{3,2,1,0:T(1,128)} %bitcast.18, f32[137,16,1,128]{3,2,1,0:T(1,128)} %bitcast.19, ...), custom_call_target="tpu_custom_call" | custom-call | tf_op jit(solution)/shard_map/pallas_call | solution.py:608
  65.8 0.0 copy-done
  65.8 0.0 copy-done.1
  65.8 1.5 %shard_map.114 = (f32[2192,128]{1,0:T(8,128)}, f32[2192,128]{1,0:T(8,128)}) custom-call(f32[1,128]{1,0:T(1,128)S(1)} %get-tuple-element.7.scale, f32[2192,128]{1,0:T(8,128)S(1)} %bitcast.16, f32[2192,128]{1,0:T(8,128)S(1)} %bitcast.14, f32[2192,128]{1,0:T(8,128)S(1)} %get-tuple-element.8.residual_dual, f32[2192,128]{1,0:T(8,128)S(1)} %get-tuple-element.9.residual_incr), custom_call_target="tpu_custom_call" | custom-call | tf_op jit(solution)/shard_map/pallas_call | solution.py:619
Async XLA Ops:
  0.6 65.1 %copy-start = (f32[1,137,16,128]{3,2,1,0:T(8,128)S(1)}, f32[1,137,16,128]{3,2,1,0:T(8,128)}, u32[]{:S(2)}) copy-start(f32[1,137,16,128]{3,2,1,0:T(8,128)} %param.10) | copy-start | bytes 3366916
  0.6 65.1 %copy-start.1 = (f32[1,137,16,128]{3,2,1,0:T(8,128)S(1)}, f32[1,137,16,128]{3,2,1,0:T(8,128)}, u32[]{:S(2)}) copy-start(f32[1,137,16,128]{3,2,1,0:T(8,128)} %param.11) | copy-start | bytes 3366916
